TPU v7x, 16 devices: a 4x2x1 block of a 4x4x8 slice. The times are simulated.
16 devices in a mesh: mp: 2 (over y, z), dp: 8 (over x, core).
Axes of the slice: x: 4, y: 2, z: 1, core: 2. Of those that a mesh axis runs over, the one named last changes fastest.
The devices are a block of a 4x4x8 slice.
Arguments:
- grad_partial: float32 [16, 1, 2048, 7168], P(('mp', 'dp')), parts along dimension 0
- momentum: float32 [2, 2048, 7168], P('mp', 'dp'), parts along dimension 0
- weight: float32 [2, 2048, 7168], P('mp', 'dp'), parts along dimension 0
Outputs:
- output 1: float32 [2, 2048, 7168], P('mp', 'dp'), parts along dimension 0
- output 2: float32 [2, 2048, 7168], P('mp', 'dp'), parts along dimension 0
- output 3: bfloat16 [2, 2048, 7168], P('mp'), parts along dimension 0
There are 2 independent parts. A program takes and returns all parts, laid end to end along the dimension named above; each array names one.
All inputs are finite; a program needn't handle non-finite values.
Results may differ from a plain program's by a relative error of at most 0.0174769.
Values are sent between devices in bfloat16 or wider.
A program may use at most 768 MiB of HBM per device.

v0:
```python
import math
import jax
import jax.numpy as jnp
from jax import lax
from jax.sharding import PartitionSpec as P

MOMENTUM = 0.95
LEARN_RATE = 2.0
WEIGHT_DECAY = 0.25
NS_STEPS = 5
COEF_A = 3.4445
COEF_B = -4.7750
COEF_C = 2.0315


def orthogonalise(update):
    num_rows, num_cols = update.shape[1], update.shape[2]
    as_float = update.astype(jnp.float32)
    sq_norm = jnp.sum(as_float * as_float, axis=(1, 2), keepdims=True)
    ortho = (as_float / (jnp.sqrt(sq_norm) + 1e-7)).astype(jnp.bfloat16)
    if num_rows <= num_cols:
        gram_form, apply_form = 'qkl,qjl->qkj', 'qkj,qjl->qkl'
    else:
        gram_form, apply_form = 'qlk,qlj->qkj', 'qkj,qlj->qlk'
    for _ in range(NS_STEPS):
        gram = jnp.einsum(gram_form, ortho, ortho, preferred_element_type=jnp.float32).astype(jnp.bfloat16)
        gram_sq = jnp.einsum('qkj,qji->qki', gram, gram, preferred_element_type=jnp.float32)
        poly = (COEF_B * gram.astype(jnp.float32) + COEF_C * gram_sq).astype(jnp.bfloat16)
        ortho = (COEF_A * ortho.astype(jnp.float32) + jnp.einsum(apply_form, poly, ortho, preferred_element_type=jnp.float32)).astype(jnp.bfloat16)
    return ortho


def solution(mesh):
    group_size = mesh.shape['dp']

    def local_step(grad_part, momentum, weight):
        grad = lax.psum_scatter(grad_part[0], 'dp', scatter_dimension=1, tiled=True) / group_size
        new_momentum = MOMENTUM * momentum + grad
        direction = (grad + MOMENTUM * new_momentum).astype(jnp.bfloat16)
        num_mats, slab_rows, num_cols = direction.shape
        num_rows = group_size * slab_rows
        num_rounds = -(-num_mats // group_size)
        padded = jnp.pad(direction, ((0, num_rounds * group_size - num_mats), (0, 0), (0, 0)))
        per_round = padded.reshape(num_rounds, group_size, slab_rows, num_cols)
        gathered = lax.all_to_all(per_round, 'dp', 1, 2, tiled=True)
        ortho_full = orthogonalise(gathered.reshape(num_rounds, num_rows, num_cols))
        returned = lax.all_to_all(ortho_full.reshape(num_rounds, 1, num_rows, num_cols), 'dp', 2, 1, tiled=True)
        ortho_slab = returned.reshape(num_rounds * group_size, slab_rows, num_cols)[:num_mats]
        scale = 0.2 * math.sqrt(max(num_rows, num_cols))
        new_weight = weight - LEARN_RATE * (scale * ortho_slab.astype(jnp.float32) + WEIGHT_DECAY * weight)
        weight_bf16 = lax.all_gather(new_weight.astype(jnp.bfloat16), 'dp', axis=1, tiled=True)
        return new_momentum, new_weight, weight_bf16

    return jax.shard_map(local_step, mesh=mesh, in_specs=(P(('mp', 'dp')), P('mp', 'dp'), P('mp', 'dp')), out_specs=(P('mp', 'dp'), P('mp', 'dp'), P('mp')), check_vma=False)
```

profile of v0, /device:TPU:113, one launch (start us, length us, event | category | flops | bytes accessed | tf_op | source)
XLA Modules:
  0.0 2403.6 jit_solution(7282748880202373791)
XLA Ops:
  8.0 289.6 %reduce-scatter.2.cloned.1.call-done = f32[1,256,7168]{2,1,0:T(8,128)} async-done(((f32[1,2048,7168]{2,1,0:T(8,128)}), f32[1,256,7168]{2,1,0:T(8,128)}) %reduce-scatter.2.cloned.1.call-update) | async-done | bytes 7340048 | tf_op jit(solution)/shard_map/reduce_scatter | solution.py:37
  318.1 329.5 %all_to_all.21 = bf16[1,8,256,7168]{3,2,0,1:T(8,128)(2,1)} all-to-all(bf16[1,8,256,7168]{3,2,0,1:T(8,128)(2,1)} %pad_bitcast_fusion), channel_id=1, replica_groups=mesh['mp'=2,'dp'=8] {'dp'}, dimensions={1} | all-to-all | bytes 58720256 | tf_op jit(solution)/shard_map/all_to_all | solution.py:45
  686.2 79.2 %fusion.12 = bf16[2048,2048]{1,0:T(8,128)(2,1)} fusion(bf16[2048,7168]{1,0:T(8,128)(2,1)} %bitcast.52), kind=kOutput, calls=%fused_computation.28 | convolution fusion | flops 60129542144 | bytes 37748736 | tf_op jit(solution)/shard_map/qkl,qjl->qkj/dot_general | solution.py:26
  765.4 24.3 %add_convert_fusion.9 = bf16[2048,2048]{1,0:T(8,128)(2,1)S(1)} fusion(bf16[2048,2048]{1,0:T(8,128)(2,1)} %fusion.12), kind=kOutput, calls=%fused_computation.15 | convolution fusion | flops 17200840704 | bytes 16777216 | tf_op jit(solution)/shard_map/qkj,qji->qki/dot_general | solution.py:27
  789.7 70.7 %add_convert_fusion.4 = bf16[2048,7168]{1,0:T(8,128)(2,1)} fusion(bf16[2048,7168]{1,0:T(8,128)(2,1)} %bitcast.53, bf16[2048,2048]{1,0:T(8,128)(2,1)S(1)} %add_convert_fusion.9), kind=kOutput, calls=%fused_computation.8 | convolution fusion | flops 60188262400 | bytes 67108864 | tf_op jit(solution)/shard_map/qkj,qjl->qkl/dot_general | solution.py:29
  860.4 79.4 %fusion.13 = bf16[2048,2048]{1,0:T(8,128)(2,1)} fusion(bf16[2048,7168]{1,0:T(8,128)(2,1)} %add_convert_fusion.4), kind=kOutput, calls=%fused_computation.29 | convolution fusion | flops 60129542144 | bytes 37748736 | tf_op jit(solution)/shard_map/qkl,qjl->qkj/dot_general | solution.py:26
  939.8 24.0 add_convert_fusion.8
  963.8 70.6 %add_convert_fusion.3 = bf16[2048,7168]{1,0:T(8,128)(2,1)} fusion(bf16[2048,7168]{1,0:T(8,128)(2,1)} %add_convert_fusion.4, bf16[2048,2048]{1,0:T(8,128)(2,1)S(1)} %add_convert_fusion.8), kind=kOutput, calls=%fused_computation.7 | convolution fusion | flops 60188262400 | bytes 67108864 | tf_op jit(solution)/shard_map/qkj,qjl->qkl/dot_general | solution.py:29
  1034.3 79.6 %fusion.14 = bf16[2048,2048]{1,0:T(8,128)(2,1)} fusion(bf16[2048,7168]{1,0:T(8,128)(2,1)} %add_convert_fusion.3), kind=kOutput, calls=%fused_computation.30 | convolution fusion | flops 60129542144 | bytes 37748736 | tf_op jit(solution)/shard_map/qkl,qjl->qkj/dot_general | solution.py:26
  1113.9 24.0 add_convert_fusion.7
  1137.9 70.8 %add_convert_fusion.2 = bf16[2048,7168]{1,0:T(8,128)(2,1)} fusion(bf16[2048,7168]{1,0:T(8,128)(2,1)} %add_convert_fusion.3, bf16[2048,2048]{1,0:T(8,128)(2,1)S(1)} %add_convert_fusion.7), kind=kOutput, calls=%fused_computation.6 | convolution fusion | flops 60188262400 | bytes 67108864 | tf_op jit(solution)/shard_map/qkj,qjl->qkl/dot_general | solution.py:29
  1208.7 79.5 %fusion.15 = bf16[2048,2048]{1,0:T(8,128)(2,1)} fusion(bf16[2048,7168]{1,0:T(8,128)(2,1)} %add_convert_fusion.2), kind=kOutput, calls=%fused_computation.31 | convolution fusion | flops 60129542144 | bytes 37748736 | tf_op jit(solution)/shard_map/qkl,qjl->qkj/dot_general | solution.py:26
  1288.2 24.0 add_convert_fusion.6
  1312.2 70.8 %add_convert_fusion.1 = bf16[2048,7168]{1,0:T(8,128)(2,1)} fusion(bf16[2048,7168]{1,0:T(8,128)(2,1)} %add_convert_fusion.2, bf16[2048,2048]{1,0:T(8,128)(2,1)S(1)} %add_convert_fusion.6), kind=kOutput, calls=%fused_computation.5 | convolution fusion | flops 60188262400 | bytes 67108864 | tf_op jit(solution)/shard_map/qkj,qjl->qkl/dot_general | solution.py:29
  1382.9 79.3 %fusion.16 = bf16[2048,2048]{1,0:T(8,128)(2,1)} fusion(bf16[2048,7168]{1,0:T(8,128)(2,1)} %add_convert_fusion.1), kind=kOutput, calls=%fused_computation.32 | convolution fusion | flops 60129542144 | bytes 37748736 | tf_op jit(solution)/shard_map/qkl,qjl->qkj/dot_general | solution.py:26
  1462.3 24.0 add_convert_fusion.5
  1486.3 70.9 %fusion.2 = bf16[1,1,2048,7168]{3,2,1,0:T(8,128)(2,1)} fusion(bf16[2048,7168]{1,0:T(8,128)(2,1)} %add_convert_fusion.1, bf16[2048,2048]{1,0:T(8,128)(2,1)S(1)} %add_convert_fusion.5), kind=kOutput, calls=%fused_computation.9 | convolution fusion | flops 60188262400 | bytes 67108864 | tf_op jit(solution)/shard_map/qkj,qjl->qkl/dot_general | solution.py:29
  1557.2 50.4 %copy.10 = bf16[1,1,2048,7168]{3,1,0,2:T(2,128)(2,1)} copy(bf16[1,1,2048,7168]{3,2,1,0:T(8,128)(2,1)} %fusion.2) | data formatting | bytes 58720256 | tf_op jit(solution)/shard_map/reshape | solution.py:47
  1608.1 173.3 %reduce.3 = bf16[2048,7168]{1,0:T(8,128)(2,1)} reduce(bf16[2048,1,1,7168]{3,2,1,0:T(2,128)(2,1)} %bitcast.48, bf16[]{:T(256)} %broadcast.78), dimensions={1,2}, to_apply=%bitcast.47.reduce_sub_computation | reduce | bytes 58720256
  1781.3 28.0 %reshape.201 = bf16[8,2,917504]{2,1,0:T(2,128)(2,1)} reshape(bf16[2048,7168]{1,0:T(8,128)(2,1)} %reduce.3) | data formatting | bytes 58720256
  1809.3 329.5 %all_to_all.22 = bf16[8,2,917504]{2,1,0:T(2,128)(2,1)} all-to-all(bf16[8,2,917504]{2,1,0:T(2,128)(2,1)} %reshape.201), channel_id=1, replica_groups=mesh['mp'=2,'dp'=8] {'dp'}, dimensions={0} | all-to-all | bytes 58720256 | tf_op jit(solution)/shard_map/all_to_all | solution.py:47
  2138.8 64.6 %reshape.202 = bf16[2048,1,1,7168]{3,2,1,0:T(2,128)(2,1)} reshape(bf16[8,2,917504]{2,1,0:T(2,128)(2,1)} %all_to_all.22) | data formatting | bytes 58720256
  2203.4 30.2 %copy.8 = bf16[1,1,2048,7168]{3,2,0,1:T(8,128)(2,1)} copy(bf16[1,1,2048,7168]{3,1,0,2:T(2,128)(2,1)} %bitcast.49) | data formatting | bytes 58720256
  2241.2 135.0 %all-gather.2.cloned.1.call-done = bf16[1,2048,7168]{2,1,0:T(8,128)(2,1)} async-done(((bf16[1,256,7168]{2,1,0:T(8,128)(2,1)}), bf16[1,2048,7168]{2,1,0:T(8,128)(2,1)}) %all-gather.2.cloned.1.call-update) | async-done | bytes 29360144 | tf_op jit(solution)/shard_map/all_gather | solution.py:51
  (11 shorter events, 87.4 us)
Async XLA Ops:
  7.2 290.5 %reduce-scatter.2.cloned.1.call-start = ((), (), s32[]{:S(2)}) async-start(), calls=%async_computation.3 | async-start | bytes 66060288 | tf_op jit(solution)/shard_map/reduce_scatter | solution.py:37
  8.0 2368.2 %all-gather.2.cloned.1.call-start = ((), (), s32[]{:S(2)}) async-start(), calls=%async_computation.4 | async-start | bytes 33030144 | tf_op jit(solution)/shard_map/all_gather | solution.py:51
Sparse Core Ops, SparseCore 0:
  10.4 287.2 reduce-scatter.1
  2241.3 134.8 all-gather.1
where the time goes:
time: 2410 us; the launch traced here: 2400 us
  matrix products  871 us (36%)
  blocking collectives  659 us (27%)
  waiting for transfers between devices  425 us (18%)
  other arithmetic  229 us (10%)
  local copies, waits for them, and re-layouts  204 us (8%)
    dot_general x5, matrix products, orthogonalise(): jnp.einsum(gram_form, ortho, ortho, preferred_element_type=jnp.float32)  397 us
    dot_general x5, matrix products, orthogonalise(): jnp.einsum(apply_form, poly, ortho, preferred_element_type=jnp.float32)  354 us
    all_to_all x1, blocking collectives, local_step(): gathered = lax.all_to_all(per_round, 'dp', 1, 2, tiled=True)  330 us
    all_to_all x1, blocking collectives, local_step(): lax.all_to_all(ortho_full.reshape(num_rounds, 1, num_rows, num_cols), 'dp...  329 us
    reduce_scatter x1, waiting for transfers between devices, local_step(): lax.psum_scatter(grad_part[0], 'dp', scatter_dimension=1, tiled=True)  290 us
    unnamed x1, other arithmetic  173 us
    unnamed x5, local copies, waits for them, and re-layouts  143 us
    all_gather x1, waiting for transfers between devices, local_step(): lax.all_gather(new_weight.astype(jnp.bfloat16), 'dp', axis=1, tiled=True)  135 us
  transfers between devices with their start and end apart: 2, of which 2 were waited for; matrix products, arithmetic and copies ran while one was open for 0% of the time, Pallas kernels for 0%

commit v1 on v0

v1 whole, which is shorter than its diff:
```python
import math
import jax
import jax.numpy as jnp
from jax import lax
from jax.experimental import pallas as pl
from jax.experimental.pallas import tpu as pltpu
from jax.sharding import PartitionSpec as P

MOMENTUM = 0.95
LEARN_RATE = 2.0
WEIGHT_DECAY = 0.25
NS_STEPS = 5
COEF_A = 3.4445
COEF_B = -4.7750
COEF_C = 2.0315

MESH = pl.DeviceIdType.MESH
F32, BF16 = jnp.float32, jnp.bfloat16
CORES = 2
BLOCK = 512
CHUNK = 512
BLOCKS = (((0, 0), (2, 0), (1, 1), (3, 1), (3, 3)), ((1, 0), (3, 0), (2, 1), (2, 2), (3, 2)))


def lookup(index, values):
    packed = 0
    for place, value in enumerate(values):
        packed += value * 4 ** place
    result = jnp.int32(values[0])
    for place, value in enumerate(values[1:], 1):
        result = jnp.where(index == place, jnp.int32(value), result)
    return result


def block_of(core, index):
    row = jnp.where(core == 0, lookup(index, [b[0] for b in BLOCKS[0]]), lookup(index, [b[0] for b in BLOCKS[1]]))
    col = jnp.where(core == 0, lookup(index, [b[1] for b in BLOCKS[0]]), lookup(index, [b[1] for b in BLOCKS[1]]))
    return row, col


def span(index, size):
    return pl.ds(pl.multiple_of(index * size, size), size)


def newton_schulz(group, rows, half, scale, u_ref, sq_ref, w_ref, wb_ref, xrow_ref, wcol_ref,
                  x_ref, gram, poly, part_out, part_in, w_tile, o_tile, norm_buf,
                  load_sem, part_send, part_recv, gram_send, gram_recv, poly_send, poly_recv,
                  w_send, w_recv, w_fwd_send, w_fwd_recv, tile_sem, out_sem, out_send, out_recv, row_sem, row_send, row_recv):
    me = lax.axis_index('dp')
    core, chip = lax.rem(me, CORES), me // CORES
    chips = group // CORES
    slab = rows // group
    partner = chip * CORES + (1 - core)
    right_chip, left_chip = lax.rem(chip + 1, chips), lax.rem(chip + chips - 1, chips)
    num_chunks = half // CHUNK
    slots = num_chunks + 1

    def remote(src, dst, send, recv, device):
        return pltpu.make_async_remote_copy(src, dst, send, recv, device_id={'dp': device}, device_id_type=MESH)

    barrier = pltpu.get_barrier_semaphore()
    peers = [partner] + [c * CORES + h for c in (right_chip, left_chip) for h in range(CORES)]
    for peer in peers:
        pl.semaphore_signal(barrier, inc=1, device_id={'dp': peer}, device_id_type=MESH)
    pl.semaphore_wait(barrier, len(peers))

    piece = slab // 2

    def w_first(side, h, part):
        to_chip = right_chip if side == 0 else left_chip
        row0 = me * slab + part * piece
        return remote(w_ref.at[pl.ds(part * piece, piece), pl.ds(h * half, half)],
                      wcol_ref.at[pl.ds(pl.multiple_of(row0, piece), piece), :],
                      w_send.at[side, h, part], w_recv.at[side, core, part], to_chip * CORES + h)

    def w_first_arrival(side, from_core, part):
        from_chip = left_chip if side == 0 else right_chip
        row0 = (from_chip * CORES + from_core) * slab + part * piece
        where = wcol_ref.at[pl.ds(pl.multiple_of(row0, piece), piece), :]
        return remote(where, where, w_send.at[side, 0, part], w_recv.at[side, from_core, part], partner)

    def w_forward(side, from_core):
        from_chip = left_chip if side == 0 else right_chip
        to_chip = right_chip if side == 0 else left_chip
        row0 = (from_chip * CORES + from_core) * slab + side * piece
        where = wcol_ref.at[pl.ds(pl.multiple_of(row0, piece), piece), :]
        return remote(where, where, w_fwd_send.at[side, from_core], w_fwd_recv.at[side, from_core], to_chip * CORES + core)

    def w_pair():
        return remote(w_ref.at[:, pl.ds(pl.multiple_of((1 - core) * half, half), half)],
                      wcol_ref.at[span(me, slab), :], tile_sem.at[3], tile_sem.at[4], partner)

    def w_own():
        return pltpu.make_async_copy(w_ref.at[:, pl.ds(pl.multiple_of(core * half, half), half)],
                                     wcol_ref.at[span(me, slab), :], tile_sem.at[2])

    loads = [pltpu.make_async_copy(u_ref.at[:, pl.ds(pl.multiple_of(core * half + c * CHUNK, CHUNK), CHUNK)], x_ref.at[c], load_sem.at[c])
             for c in range(num_chunks)]
    norm_load = pltpu.make_async_copy(sq_ref, norm_buf, load_sem.at[num_chunks])
    norm_load.start()
    for load in loads:
        load.start()
    for part in (0, 1):
        for side in (0, 1):
            for h in range(CORES):
                w_first(side, h, part if side == 0 else 1 - part).start()
    w_pair().start()
    w_own().start()
    norm_load.wait()
    inverse = 1.0 / (jnp.sqrt(norm_buf[0:1, 0:1]) + 1e-7)
    for c in range(num_chunks):
        loads[c].wait()

        def scale_rows(i, _, c=c):
            r = span(i, 256)
            x_ref[c, r, :] = (x_ref[c, r, :].astype(F32) * inverse).astype(BF16)
            return 0
        lax.fori_loop(0, rows // 256, scale_rows, 0)

    def slot_of(c, t):
        return lax.rem(c + 2 * slots - t, slots)

    def gram_send_copy(b, index, row, col):
        return remote(gram.at[span(row, BLOCK), span(col, BLOCK)], gram.at[span(row, BLOCK), span(col, BLOCK)],
                      gram_send.at[index, b], gram_recv.at[index, b], partner)

    def poly_send_copy(b, index, row, col):
        return remote(poly.at[span(row, BLOCK), span(col, BLOCK)], poly.at[span(row, BLOCK), span(col, BLOCK)],
                      poly_send.at[index, b], poly_recv.at[index, b], partner)

    def both(copy, owner, index, act):
        row, col = block_of(owner, index)
        act(copy(0, index, row, col))

        @pl.when(row != col)
        def _():
            act(copy(1, index, col, row))

    def part_copy(index):
        return remote(part_out.at[index], part_in.at[index], part_send.at[index], part_recv.at[index], partner)

    def step(t, _):
        def gram_block(row, col):
            ri, rj = span(row, BLOCK), span(col, BLOCK)
            xi = jnp.concatenate([x_ref[slot_of(c, t), ri, :] for c in range(num_chunks)], axis=1)
            xj = jnp.concatenate([x_ref[slot_of(c, t), rj, :] for c in range(num_chunks)], axis=1)
            return lax.dot_general(xi, xj, (((1,), (1,)), ((), ())), preferred_element_type=F32)

        @pl.when(t == 2)
        def _():
            for side in (0, 1):
                for from_core in range(CORES):
                    w_first_arrival(side, from_core, side).wait_recv()
                    w_forward(side, from_core).start()

        def gram_step(index, _):
            owner = jnp.where(index < 5, 1 - core, core)
            place = lax.rem(index, 5)
            row, col = block_of(owner, place)
            value = gram_block(row, col)

            @pl.when(index < 5)
            def _():
                part_out[place] = value
                part_copy(place).start()

            @pl.when(index >= 5)
            def _():
                part_copy(place).wait_recv()
                block = (value + part_in[place]).astype(BF16)
                gram[span(row, BLOCK), span(col, BLOCK)] = block

                @pl.when(row != col)
                def _():
                    gram[span(col, BLOCK), span(row, BLOCK)] = block.T
                both(gram_send_copy, core, place, lambda cp: cp.start())
            return 0
        lax.fori_loop(0, 10, gram_step, 0)

        def poly_step(index, _):
            @pl.when(index == 0)
            def _():
                for i in range(4):
                    both(gram_send_copy, 1 - core, i, lambda cp: cp.wait_recv())

            @pl.when(index == 1)
            def _():
                both(gram_send_copy, 1 - core, 4, lambda cp: cp.wait_recv())
            row, col = block_of(core, index)
            ri, rj = span(row, BLOCK), span(col, BLOCK)
            square = jnp.dot(gram[ri, :], gram[:, rj], preferred_element_type=F32)
            block = (COEF_B * gram[ri, rj].astype(F32) + COEF_C * square).astype(BF16)
            poly[ri, rj] = block

            @pl.when(row != col)
            def _():
                poly[rj, ri] = block.T
            both(poly_send_copy, core, index, lambda cp: cp.start())
            return 0
        lax.fori_loop(0, 5, poly_step, 0)

        tall = 1024

        def poly_waits(q):
            @pl.when(q == 0)
            def _():
                for i in range(4):
                    both(poly_send_copy, 1 - core, i, lambda cp: cp.wait_recv())

            @pl.when(q == 1)
            def _():
                both(poly_send_copy, 1 - core, 4, lambda cp: cp.wait_recv())

        def apply_block(q):
            c, m = q // 2, lax.rem(q, 2)
            rm = span(m, tall)
            src, dst = slot_of(c, t), slot_of(c, t + 1)
            total = jnp.dot(poly[rm, :], x_ref[src], preferred_element_type=F32)
            return c, m, rm, dst, (COEF_A * x_ref[src, rm, :].astype(F32) + total).astype(BF16)

        @pl.when(t < NS_STEPS - 1)
        def _():
            def apply_step(q, _):
                poly_waits(q)
                c, m, rm, dst, value = apply_block(q)
                x_ref[dst, rm, :] = value
                return 0
            lax.fori_loop(0, 2 * num_chunks, apply_step, 0)

        @pl.when(t == NS_STEPS - 1)
        def _():
            for side in (0, 1):
                for from_core in range(CORES):
                    w_first_arrival(side, from_core, 1 - side).wait_recv()
                    w_forward(side, from_core).wait_recv()
            w_pair().wait_recv()
            w_own().wait()

            def tile_load(q):
                c, m = q // 2, lax.rem(q, 2)
                return pltpu.make_async_copy(wcol_ref.at[span(m, tall), span(c, CHUNK)], w_tile.at[lax.rem(q, 2)], tile_sem.at[lax.rem(q, 2)])

            def out_pair(q, slot):
                c, m = q // 2, lax.rem(q, 2)
                where = wb_ref.at[span(m, tall), pl.ds(pl.multiple_of(core * half + c * CHUNK, CHUNK), CHUNK)]
                return (pltpu.make_async_copy(o_tile.at[slot], where, out_sem.at[slot]),
                        remote(o_tile.at[slot], where, out_send.at[slot], out_recv.at[q], partner))

            def row_pair(c):
                slot = slot_of(c, t + 1)
                cols = pl.ds(pl.multiple_of(core * half + c * CHUNK, CHUNK), CHUNK)
                return (pltpu.make_async_copy(x_ref.at[slot, span(me, slab), :], xrow_ref.at[:, cols], row_sem.at[c]),
                        remote(x_ref.at[slot, span(partner, slab), :], xrow_ref.at[:, cols], row_send.at[c], row_recv.at[c], partner))

            tile_load(0).start()

            def last_step(q, _):
                poly_waits(q)

                @pl.when(q + 1 < 2 * num_chunks)
                def _():
                    tile_load(q + 1).start()
                c, m, rm, dst, value = apply_block(q)
                x_ref[dst, rm, :] = value
                slot = lax.rem(q, 2)
                tile_load(q).wait()

                @pl.when(q >= 2)
                def _():
                    here, there = out_pair(q - 2, slot)
                    here.wait()
                    there.wait_send()
                old = w_tile[slot]
                new = old - LEARN_RATE * (scale * value.astype(F32) + WEIGHT_DECAY * old)
                o_tile[slot] = new.astype(BF16)
                here, there = out_pair(q, slot)
                here.start()
                there.start()

                @pl.when(m == 1)
                def _():
                    here, there = row_pair(c)
                    here.start()
                    there.start()
                return 0
            lax.fori_loop(0, 2 * num_chunks, last_step, 0)
            for q in (2 * num_chunks - 2, 2 * num_chunks - 1):
                here, there = out_pair(q, q % 2)
                here.wait()
                there.wait_send()

            def out_arrival(q, _):
                c, m = q // 2, lax.rem(q, 2)
                where = wb_ref.at[span(m, tall), pl.ds(pl.multiple_of((1 - core) * half + c * CHUNK, CHUNK), CHUNK)]
                remote(o_tile.at[0], where, out_send.at[0], out_recv.at[q], partner).wait_recv()
                return 0
            lax.fori_loop(0, 2 * num_chunks, out_arrival, 0)

            def row_end(c, _):
                here, there = row_pair(c)
                here.wait()
                there.wait()
                return 0
            lax.fori_loop(0, num_chunks, row_end, 0)

        def drain(i, _):
            part_copy(i).wait_send()
            both(gram_send_copy, core, i, lambda cp: cp.wait_send())
            both(poly_send_copy, core, i, lambda cp: cp.wait_send())
            return 0
        lax.fori_loop(0, 5, drain, 0)
        return 0
    lax.fori_loop(0, NS_STEPS, step, 0)

    for part in (0, 1):
        for side in (0, 1):
            for h in range(CORES):
                w_first(side, h, part).wait_send()
    for side in (0, 1):
        for from_core in range(CORES):
            w_forward(side, from_core).wait_send()
    w_pair().wait_send()


def solution(mesh):
    group = mesh.shape['dp']

    def orthogonal_update(direction, sq_norm, weight):
        slab, num_cols = weight.shape
        rows = slab * group
        half = num_cols // CORES
        scale = 0.2 * math.sqrt(max(rows, num_cols))
        num_chunks = half // CHUNK
        anywhere = pl.BlockSpec(memory_space=pl.ANY)
        dma = pltpu.SemaphoreType.DMA

        def kernel(*refs):
            newton_schulz(group, rows, half, scale, *refs)
        shape = jax.ShapeDtypeStruct
        return pl.pallas_call(
            kernel,
            name='newton_schulz',
            out_shape=(shape((rows, num_cols), BF16), shape((slab, num_cols), BF16), shape((rows, half), F32)),
            in_specs=[anywhere] * 3,
            out_specs=(anywhere,) * 3,
            scratch_shapes=[
                pltpu.VMEM((num_chunks + 1, rows, CHUNK), BF16),
                pltpu.VMEM((rows, rows), BF16),
                pltpu.VMEM((rows, rows), BF16),
                pltpu.VMEM((5, BLOCK, BLOCK), F32),
                pltpu.VMEM((5, BLOCK, BLOCK), F32),
                pltpu.VMEM((2, 1024, CHUNK), F32),
                pltpu.VMEM((2, 1024, CHUNK), BF16),
                pltpu.VMEM((8, 128), F32),
                dma((num_chunks + 1,)),
                dma((5,)), dma((5,)), dma((5, 2)), dma((5, 2)), dma((5, 2)), dma((5, 2)),
                dma((2, 2, 2)), dma((2, 2, 2)), dma((2, 2)), dma((2, 2)),
                dma((5,)),
                dma((2,)), dma((2,)), dma((2 * num_chunks,)),
                dma((num_chunks,)), dma((num_chunks,)), dma((num_chunks,)),
            ],
            compiler_params=pltpu.CompilerParams(collective_id=1, has_side_effects=True, vmem_limit_bytes=60 * 2 ** 20),
        )(direction, sq_norm, weight)

    def local_step(grad_part, momentum, weight):
        grad = lax.psum_scatter(grad_part[0], 'dp', scatter_dimension=1, tiled=True) / group
        new_momentum = MOMENTUM * momentum + grad
        direction = (grad + MOMENTUM * new_momentum).astype(BF16)
        as_float = direction.astype(F32)
        sq_norm = lax.psum(jnp.sum(as_float * as_float), 'dp')
        whole = lax.all_gather(direction[0], 'dp', axis=0, tiled=True)
        weight_bf16, ortho, _ = orthogonal_update(whole, jnp.full((8, 128), sq_norm, F32), weight[0])
        scale = 0.2 * math.sqrt(max(weight_bf16.shape))
        new_weight = weight - LEARN_RATE * (scale * ortho[None].astype(F32) + WEIGHT_DECAY * weight)
        return new_momentum, new_weight, weight_bf16[None]

    return jax.shard_map(local_step, mesh=mesh, in_specs=(P(('mp', 'dp')), P('mp', 'dp'), P('mp', 'dp')), out_specs=(P('mp', 'dp'), P('mp', 'dp'), P('mp')), check_vma=False)
```

time: 2410 us -> 823 us (0.34)
  matrix products: 871 us -> 0 us
  blocking collectives: 659 us -> 13.4 us
  Pallas kernels: 0 us -> 343 us
  other arithmetic: 229 us -> 18 us
  local copies, waits for them, and re-layouts: 204 us -> 21.4 us
    dot_general x15 -> x0, matrix products: 871 us -> none  [the longest x5 397 us: orthogonalise(): jnp.einsum(gram_form, ortho, ortho, preferred_element_type=jnp.float32)]
    all_to_all x2 -> x0, blocking collectives: 659 us -> none  [the longest x1 330 us: local_step(): gathered = lax.all_to_all(per_round, 'dp', 1, 2, tiled=True)]
    pallas_call x0 -> x1, Pallas kernels: none -> 343 us  [orthogonal_update(): pl.pallas_call(kernel, name='newton_schulz', out_shape=(shape((rows, num_...]
    unnamed x1 -> x0, other arithmetic: 173 us -> none
    unnamed x5 -> x1, local copies, waits for them, and re-layouts: 143 us -> 20.1 us
    reshape x2 -> x0, local copies, waits for them, and re-layouts: 60.3 us -> none  [the longest x1 50.4 us: local_step(): ortho_full.reshape(num_rounds, 1, num_rows, num_cols)]
    convert_element_type x3 -> x0, other arithmetic: 38.5 us -> none  [the longest x1 20.4 us: orthogonalise(): ortho = (as_float / (jnp.sqrt(sq_norm) + 1e-07)).astype(jnp.bfloat16)]
where the time goes in v1:
time: 823 us
  waiting for transfers between devices  412 us (50%)
  Pallas kernels  343 us (42%)
  local copies, waits for them, and re-layouts  21.4 us (3%)
  other arithmetic  18 us (2%)
  between operations  14.1 us (2%)
  blocking collectives  13.4 us (2%)
    pallas_call x1, Pallas kernels, orthogonal_update(): pl.pallas_call(kernel, name='newton_schulz', out_shape=(shape((rows, num_...  343 us
    reduce_scatter x1, waiting for transfers between devices, local_step(): lax.psum_scatter(grad_part[0], 'dp', scatter_dimension=1, tiled=True)  290 us
    all_gather x1, waiting for transfers between devices, local_step(): whole = lax.all_gather(direction[0], 'dp', axis=0, tiled=True)  122 us
    unnamed x1, local copies, waits for them, and re-layouts  20.1 us
  transfers between devices with their start and end apart: 2, of which 2 were waited for; matrix products, arithmetic and copies ran while one was open for 0% of the time, Pallas kernels for 0%

profile of v1, /device:TPU:113, one launch (start us, length us, event | category | flops | bytes accessed | tf_op | source)
XLA Modules:
  0.0 822.6 jit_solution(5719631876941723005)
XLA Ops:
  7.2 0.1 reduce-scatter.2.cloned.1.call-start
  7.2 0.7 reduce-scatter.2.cloned.1.call-update
  8.0 0.1 all-gather.3.cloned.1.call-start
  8.0 289.6 %reduce-scatter.2.cloned.1.call-done = f32[1,256,7168]{2,1,0:T(8,128)} async-done(((f32[1,2048,7168]{2,1,0:T(8,128)}), f32[1,256,7168]{2,1,0:T(8,128)}) %reduce-scatter.2.cloned.1.call-update) | async-done | bytes 7340048 | tf_op jit(solution)/shard_map/reduce_scatter | solution.py:366
  297.7 9.3 %multiply_reduce_fusion = (f32[]{:T(128)}, bf16[1,256,7168]{2,1,0:T(8,128)(2,1)}, f32[1,256,7168]{2,1,0:T(8,128)}) fusion(f32[1,256,7168]{2,1,0:T(8,128)} %reduce-scatter.2.cloned.1.call-done, f32[1,256,7168]{2,1,0:T(8,128)} %param.4), kind=kLoop, calls=%fused_computation.3 | loop fusion | flops 16515071 | bytes 25690116 | tf_op jit(solution)/shard_map/reduce_sum | solution.py:370
  307.0 0.1 all-gather.3.cloned.1.call-update
  307.0 13.4 %psum.7 = f32[]{:T(128)} all-reduce(f32[]{:T(128)} %get-tuple-element.7), channel_id=1, replica_groups=mesh['mp'=2,'dp'=8] {'dp'}, use_global_device_ids=true, to_apply=%region_2.0 | all-reduce | flops 1 | bytes 8 | tf_op jit(solution)/shard_map/psum | solution.py:370
  320.4 121.9 %all-gather.3.cloned.1.call-done = bf16[1,2048,7168]{2,1,0:T(8,128)(2,1)} async-done(((bf16[1,256,7168]{2,1,0:T(8,128)(2,1)}), bf16[1,2048,7168]{2,1,0:T(8,128)(2,1)}) %all-gather.3.cloned.1.call-update) | async-done | bytes 29360144 | tf_op jit(solution)/shard_map/all_gather | solution.py:371
  442.4 1.2 broadcast_in_dim.7.refs_1_
  443.6 343.3 %newton_schulz.1 = (bf16[2048,7168]{1,0:T(8,128)(2,1)}, bf16[256,7168]{1,0:T(8,128)(2,1)}, f32[2048,3584]{1,0:T(8,128)}) custom-call(bf16[2048,7168]{1,0:T(8,128)(2,1)} %bitcast.13, f32[8,128]{1,0:T(8,128)} %broadcast_in_dim.7.refs_1_, f32[256,7168]{1,0:T(8,128)} %bitcast.11), custom_call_target="tpu_custom_call" | custom-call | tf_op jit(solution)/shard_map/newton_schulz/pallas_call | solution.py:340
  787.0 8.7 %fusion.1 = f32[1,256,7168]{2,1,0:T(8,128)} fusion(f32[1,256,7168]{2,1,0:T(8,128)} %param.5, bf16[256,7168]{1,0:T(8,128)(2,1)} %get-tuple-element.5), kind=kLoop, calls=%fused_computation.2 | loop fusion | flops 11010048 | bytes 18350080 | tf_op jit(solution)/shard_map/sub | solution.py:374
  795.6 20.1 %copy.7 = bf16[1,2048,7168]{2,1,0:T(8,128)(2,1)} copy(bf16[1,2048,7168]{2,1,0:T(8,128)(2,1)} %bitcast.12) | data formatting | bytes 58720256
Async XLA Ops:
  7.2 290.5 %reduce-scatter.2.cloned.1.call-start = ((), (), s32[]{:S(2)}) async-start(), calls=%async_computation.1 | async-start | bytes 66060288 | tf_op jit(solution)/shard_map/reduce_scatter | solution.py:366
  8.0 434.4 %all-gather.3.cloned.1.call-start = ((), (), s32[]{:S(2)}) async-start(), calls=%async_computation.2 | async-start | bytes 33030144 | tf_op jit(solution)/shard_map/all_gather | solution.py:371
Sparse Core Ops, SparseCore 0:
  10.4 287.2 reduce-scatter.1
  307.1 135.1 all-gather.2

commit v2 on v1

--- a/solution.py
+++ b/solution.py
@@ -19,13 +19,12 @@
 CORES = 2
 BLOCK = 512
 CHUNK = 512
+PIECE = 32
+DEPTH = 4
 BLOCKS = (((0, 0), (2, 0), (1, 1), (3, 1), (3, 3)), ((1, 0), (3, 0), (2, 1), (2, 2), (3, 2)))
 
 
 def lookup(index, values):
-    packed = 0
-    for place, value in enumerate(values):
-        packed += value * 4 ** place
     result = jnp.int32(values[0])
     for place, value in enumerate(values[1:], 1):
         result = jnp.where(index == place, jnp.int32(value), result)
@@ -42,80 +41,246 @@
     return pl.ds(pl.multiple_of(index * size, size), size)
 
 
-def newton_schulz(group, rows, half, scale, u_ref, sq_ref, w_ref, wb_ref, xrow_ref, wcol_ref,
-                  x_ref, gram, poly, part_out, part_in, w_tile, o_tile, norm_buf,
-                  load_sem, part_send, part_recv, gram_send, gram_recv, poly_send, poly_recv,
-                  w_send, w_recv, w_fwd_send, w_fwd_recv, tile_sem, out_sem, out_send, out_recv, row_sem, row_send, row_recv):
+def muon(group, rows, half, scale, grad_ref, mom_ref, w_ref, wb_ref, xrow_ref, nmom_ref, wcol_ref, pair_ref, arrived_ref,
+         x_ref, gram, poly, part_out, part_in, o_tile, tiles, stage, own, square_acc, sq_out, sq_in,
+         pair_send, pair_recv, rs_send, rs_recv, in_sem, sq_send, sq_recv, up_send, up_recv, mate_send, mate_recv, pass_send, pass_recv,
+         part_send, part_recv, gram_send, gram_recv, poly_send, poly_recv,
+         w_send, w_recv, w_fwd_send, w_fwd_recv, tile_sem, out_sem, out_send, out_recv, row_sem, row_send, row_recv):
     me = lax.axis_index('dp')
     core, chip = lax.rem(me, CORES), me // CORES
     chips = group // CORES
     slab = rows // group
     partner = chip * CORES + (1 - core)
-    right_chip, left_chip = lax.rem(chip + 1, chips), lax.rem(chip + chips - 1, chips)
+    side_chip = (lax.rem(chip + 1, chips), lax.rem(chip + chips - 1, chips))
+    far_chip = lax.rem(chip + 2, chips)
     num_chunks = half // CHUNK
     slots = num_chunks + 1
+    pieces = slab // PIECE
 
     def remote(src, dst, send, recv, device):
         return pltpu.make_async_remote_copy(src, dst, send, recv, device_id={'dp': device}, device_id_type=MESH)
 
     barrier = pltpu.get_barrier_semaphore()
-    peers = [partner] + [c * CORES + h for c in (right_chip, left_chip) for h in range(CORES)]
-    for peer in peers:
-        pl.semaphore_signal(barrier, inc=1, device_id={'dp': peer}, device_id_type=MESH)
-    pl.semaphore_wait(barrier, len(peers))
+    for other in range(1, group):
+        pl.semaphore_signal(barrier, inc=1, device_id={'dp': lax.rem(me + other, group)}, device_id_type=MESH)
+    pl.semaphore_wait(barrier, group - 1)
+
+    def dest_chip(order):
+        return jnp.where(order == 0, far_chip, jnp.where(order == 1, side_chip[0], jnp.where(order == 2, side_chip[1], chip)))
+
+    def piece_rows(chip_index, core_index, j):
+        return pl.ds(pl.multiple_of((chip_index * CORES + core_index) * slab + j * PIECE, PIECE), PIECE)
+
+    def pair_copy(i):
+        order, j = i // pieces, lax.rem(i, pieces)
+        return remote(grad_ref.at[piece_rows(dest_chip(order), 1 - core, j), :], pair_ref.at[order, span(j, PIECE), :],
+                      pair_send.at[i], pair_recv.at[i], partner)
+
+    def pair_start(i, _):
+        pair_copy(i).start()
+        return 0
+    lax.fori_loop(0, chips * pieces, pair_start, 0)
+
+    def columns(which):
+        return pl.ds(which * half, half)
+
+    def grad_loads(order, j, col, base):
+        return (pltpu.make_async_copy(grad_ref.at[piece_rows(dest_chip(order), core, j), col], tiles.at[base], in_sem.at[base]),
+                pltpu.make_async_copy(pair_ref.at[order, span(j, PIECE), col], tiles.at[base + 1], in_sem.at[base + 1]))
+
+    def arrived_load(phase, side, j, base):
+        return pltpu.make_async_copy(arrived_ref.at[phase, side, span(j, PIECE), :], tiles.at[base], in_sem.at[base])
+
+    def rs_copy(q, side):
+        phase, j = q // pieces, lax.rem(q, pieces)
+        slot = lax.rem(q, DEPTH)
+        return remote(stage.at[side, slot], arrived_ref.at[phase, side, span(j, PIECE), :],
+                      rs_send.at[side, slot], rs_recv.at[phase, side, j], side_chip[side] * CORES + core)
+
+    def up_copy(side, h, j, sender=None):
+        where = x_ref.at[pl.ds(0, num_chunks), pl.ds(pl.multiple_of(me * slab + j * PIECE, PIECE), PIECE), :]
+        return remote(own.at[pl.ds(h * num_chunks, num_chunks), span(j, PIECE), :], where,
+                      up_send.at[side, h, j], up_recv.at[side, core if sender is None else sender, j], side_chip[side] * CORES + h)
+
+    def mate_copy(j):
+        where = x_ref.at[pl.ds(0, num_chunks), pl.ds(pl.multiple_of(me * slab + j * PIECE, PIECE), PIECE), :]
+        return remote(own.at[pl.ds((1 - core) * num_chunks, num_chunks), span(j, PIECE), :], where,
+                      mate_send.at[j], mate_recv.at[j], partner)
+
+    def nmom_copy(j, which):
+        return pltpu.make_async_copy(tiles.at[5], nmom_ref.at[span(j, PIECE), columns(which)], in_sem.at[5])
+
+    square_acc[...] = jnp.zeros_like(square_acc)
+
+    def send_sums(q):
+        phase, j = q // pieces, lax.rem(q, pieces)
+
+        @pl.when(phase == 0)
+        def _():
+            pair_copy(j).wait_recv()
+
+        @pl.when(phase == 1)
+        def _():
+            pair_copy(pieces + j).wait_recv()
+            pair_copy(2 * pieces + j).wait_recv()
+        for side in (0, 1):
+            order = jnp.where(phase == 0, 0, 1 + side)
+            which = jnp.where(phase == 1, 1 - side, side)
+            col = pl.ds(pl.multiple_of(which * half, half), half)
+            loads = grad_loads(order, j, col, 3 * side)
+            for load in loads:
+                load.start()
+
+            @pl.when(phase == 2)
+            def _():
+                rs_copy(j, side).wait_recv()
+                arrived_load(0, side, j, 3 * side + 2).start()
+
+        for side in (0, 1):
+            slot = lax.rem(q, DEPTH)
+
+            @pl.when(q >= DEPTH)
+            def _():
+                rs_copy(q - DEPTH, side).wait_send()
+            order = jnp.where(phase == 0, 0, 1 + side)
+            which = jnp.where(phase == 1, 1 - side, side)
+            col = pl.ds(pl.multiple_of(which * half, half), half)
+            for load in grad_loads(order, j, col, 3 * side):
+                load.wait()
+
+            @pl.when(phase == 2)
+            def _():
+                arrived_load(0, side, j, 3 * side + 2).wait()
+                stage[side, slot] = (tiles[3 * side] + tiles[3 * side + 1]) + tiles[3 * side + 2]
+
+            @pl.when(phase != 2)
+            def _():
+                stage[side, slot] = tiles[3 * side] + tiles[3 * side + 1]
+            rs_copy(q, side).start()
+
+    def finish(j):
+        pair_copy(3 * pieces + j).wait_recv()
+        for which in (0, 1):
+            loads = list(grad_loads(3, j, columns(which), 0))
+            for side in (0, 1):
+                phase = 2 if side == which else 1
+                rs_copy(phase * pieces + j, side).wait_recv()
+                loads.append(arrived_load(phase, side, j, 2 + side))
+            loads.append(pltpu.make_async_copy(mom_ref.at[span(j, PIECE), columns(which)], tiles.at[4], in_sem.at[4]))
+            for load in loads:
+                load.start()
+            for load in loads:
+                load.wait()
+            if which == 1:
+                nmom_copy(j, 0).wait()
+            mean = (((tiles[0] + tiles[1]) + tiles[2]) + tiles[3]) / group
+            momentum = MOMENTUM * tiles[4] + mean
+            tiles[5] = momentum
+            nmom_copy(j, which).start()
+            update = (mean + MOMENTUM * momentum).astype(BF16)
+            for c in range(num_chunks):
+                own[which * num_chunks + c, span(j, PIECE), :] = update[:, c * CHUNK:(c + 1) * CHUNK]
+            as_float = update.astype(F32)
+            square_acc[...] += jnp.sum((as_float * as_float).reshape(PIECE // 8, 8, half), axis=0)
+        nmom_copy(j, 1).wait()
+        for side in (0, 1):
+            for h in range(CORES):
+                up_copy(side, h, j).start()
+        mate_copy(j).start()
+
+    def reduce_step(q, _):
+        @pl.when(q < 3 * pieces)
+        def _():
+            send_sums(q)
+
+        @pl.when(q >= 2 * pieces + DEPTH)
+        def _():
+            finish(q - 2 * pieces - DEPTH)
+        return 0
+    lax.fori_loop(0, 3 * pieces + DEPTH, reduce_step, 0)
+    for side in (0, 1):
+        for last in range(DEPTH):
+            rs_copy(3 * pieces - DEPTH + last, side).wait_send()
+
+    total = jnp.sum(square_acc[...])
+    sq_out[...] = jnp.full(sq_out.shape, total, F32)
+    sq_in[me] = jnp.full(sq_out.shape, total, F32)
+
+    def sq_copy(other):
+        return remote(sq_out, sq_in.at[me], sq_send.at[other], sq_recv.at[other], lax.rem(me + other, group))
+    for other in range(1, group):
+        sq_copy(other).start()
+    for other in range(1, group):
+        sq_copy(other).wait()
+    square = sq_in[0, 0:1, 0:1]
+    for i in range(1, group):
+        square = square + sq_in[i, 0:1, 0:1]
+    inverse = 1.0 / (jnp.sqrt(square) + 1e-7)
+
+    def normalise(row0, size):
+        r = pl.ds(pl.multiple_of(row0, size), size)
+        x_ref[0:num_chunks, r, :] = (x_ref[0:num_chunks, r, :].astype(F32) * inverse).astype(BF16)
+
+    def normalise_own(j, _):
+        r = pl.ds(pl.multiple_of(me * slab + j * PIECE, PIECE), PIECE)
+        x_ref[0:num_chunks, r, :] = (own[pl.ds(core * num_chunks, num_chunks), span(j, PIECE), :].astype(F32) * inverse).astype(BF16)
+        return 0
+    lax.fori_loop(0, pieces, normalise_own, 0)
+
+    def normalise_mate(j, _):
+        mate_copy(j).wait_recv()
+        normalise(partner * slab + j * PIECE, PIECE)
+        return 0
+    lax.fori_loop(0, pieces, normalise_mate, 0)
+
+    def pass_copy(side, from_core, j):
+        row0 = (side_chip[1 - side] * CORES + from_core) * slab + (side * (pieces // 2) + j) * PIECE
+        where = x_ref.at[pl.ds(0, num_chunks), pl.ds(pl.multiple_of(row0, PIECE), PIECE), :]
+        return remote(where, where, pass_send.at[side, from_core, j], pass_recv.at[side, from_core, j], side_chip[side] * CORES + core)
+
+    def arrive(j, _):
+        for side in (0, 1):
+            for from_core in range(CORES):
+                up_copy(side, core, j, from_core).wait_recv()
+                normalise((side_chip[1 - side] * CORES + from_core) * slab + j * PIECE, PIECE)
+
+                @pl.when(j // (pieces // 2) == side)
+                def _():
+                    pass_copy(side, from_core, j - side * (pieces // 2)).start()
+        return 0
+    lax.fori_loop(0, pieces, arrive, 0)
 
     piece = slab // 2
 
-    def w_first(side, h, part):
-        to_chip = right_chip if side == 0 else left_chip
-        row0 = me * slab + part * piece
+    def w_first(side, h, part, sender=None):
         return remote(w_ref.at[pl.ds(part * piece, piece), pl.ds(h * half, half)],
-                      wcol_ref.at[pl.ds(pl.multiple_of(row0, piece), piece), :],
-                      w_send.at[side, h, part], w_recv.at[side, core, part], to_chip * CORES + h)
-
-    def w_first_arrival(side, from_core, part):
-        from_chip = left_chip if side == 0 else right_chip
-        row0 = (from_chip * CORES + from_core) * slab + part * piece
-        where = wcol_ref.at[pl.ds(pl.multiple_of(row0, piece), piece), :]
-        return remote(where, where, w_send.at[side, 0, part], w_recv.at[side, from_core, part], partner)
+                      wcol_ref.at[chip, pl.ds(pl.multiple_of(core * slab + part * piece, piece), piece), :],
+                      w_send.at[side, h, part], w_recv.at[side, core if sender is None else sender, part], side_chip[side] * CORES + h)
 
     def w_forward(side, from_core):
-        from_chip = left_chip if side == 0 else right_chip
-        to_chip = right_chip if side == 0 else left_chip
-        row0 = (from_chip * CORES + from_core) * slab + side * piece
-        where = wcol_ref.at[pl.ds(pl.multiple_of(row0, piece), piece), :]
-        return remote(where, where, w_fwd_send.at[side, from_core], w_fwd_recv.at[side, from_core], to_chip * CORES + core)
+        where = wcol_ref.at[side_chip[1 - side], pl.ds(from_core * slab + side * piece, piece), :]
+        return remote(where, where, w_fwd_send.at[side, from_core], w_fwd_recv.at[side, from_core], side_chip[side] * CORES + core)
 
     def w_pair():
         return remote(w_ref.at[:, pl.ds(pl.multiple_of((1 - core) * half, half), half)],
-                      wcol_ref.at[span(me, slab), :], tile_sem.at[3], tile_sem.at[4], partner)
+                      wcol_ref.at[chip, pl.ds(pl.multiple_of(core * slab, slab), slab), :], tile_sem.at[3], tile_sem.at[4], partner)
 
     def w_own():
         return pltpu.make_async_copy(w_ref.at[:, pl.ds(pl.multiple_of(core * half, half), half)],
-                                     wcol_ref.at[span(me, slab), :], tile_sem.at[2])
-
-    loads = [pltpu.make_async_copy(u_ref.at[:, pl.ds(pl.multiple_of(core * half + c * CHUNK, CHUNK), CHUNK)], x_ref.at[c], load_sem.at[c])
-             for c in range(num_chunks)]
-    norm_load = pltpu.make_async_copy(sq_ref, norm_buf, load_sem.at[num_chunks])
-    norm_load.start()
-    for load in loads:
-        load.start()
+                                     wcol_ref.at[chip, pl.ds(pl.multiple_of(core * slab, slab), slab), :], tile_sem.at[2])
     for part in (0, 1):
         for side in (0, 1):
             for h in range(CORES):
                 w_first(side, h, part if side == 0 else 1 - part).start()
     w_pair().start()
     w_own().start()
-    norm_load.wait()
-    inverse = 1.0 / (jnp.sqrt(norm_buf[0:1, 0:1]) + 1e-7)
-    for c in range(num_chunks):
-        loads[c].wait()
-
-        def scale_rows(i, _, c=c):
-            r = span(i, 256)
-            x_ref[c, r, :] = (x_ref[c, r, :].astype(F32) * inverse).astype(BF16)
-            return 0
-        lax.fori_loop(0, rows // 256, scale_rows, 0)
+
+    def late(j, _):
+        for side in (0, 1):
+            for from_core in range(CORES):
+                pass_copy(side, from_core, j).wait()
+        return 0
+    lax.fori_loop(0, pieces // 2, late, 0)
 
     def slot_of(c, t):
         return lax.rem(c + 2 * slots - t, slots)
@@ -150,7 +315,7 @@
         def _():
             for side in (0, 1):
                 for from_core in range(CORES):
-                    w_first_arrival(side, from_core, side).wait_recv()
+                    w_first(side, 0, side, from_core).wait_recv()
                     w_forward(side, from_core).start()
 
         def gram_step(index, _):
@@ -199,6 +364,10 @@
             return 0
         lax.fori_loop(0, 5, poly_step, 0)
 
+        def part_drain(i, _):
+            part_copy(i).wait_send()
+            return 0
+        lax.fori_loop(0, 5, part_drain, 0)
         tall = 1024
 
         def poly_waits(q):
@@ -231,14 +400,14 @@
         def _():
             for side in (0, 1):
                 for from_core in range(CORES):
-                    w_first_arrival(side, from_core, 1 - side).wait_recv()
+                    w_first(side, 0, 1 - side, from_core).wait_recv()
                     w_forward(side, from_core).wait_recv()
             w_pair().wait_recv()
             w_own().wait()
 
             def tile_load(q):
                 c, m = q // 2, lax.rem(q, 2)
-                return pltpu.make_async_copy(wcol_ref.at[span(m, tall), span(c, CHUNK)], w_tile.at[lax.rem(q, 2)], tile_sem.at[lax.rem(q, 2)])
+                return pltpu.make_async_copy(wcol_ref.at[pl.ds(2 * m, 2), :, span(c, CHUNK)], part_out.at[pl.ds(2 * lax.rem(q, 2), 2)], tile_sem.at[lax.rem(q, 2)])
 
             def out_pair(q, slot):
                 c, m = q // 2, lax.rem(q, 2)
@@ -270,7 +439,7 @@
                     here, there = out_pair(q - 2, slot)
                     here.wait()
                     there.wait_send()
-                old = w_tile[slot]
+                old = part_out[pl.ds(2 * slot, 2)].reshape(tall, CHUNK)
                 new = old - LEARN_RATE * (scale * value.astype(F32) + WEIGHT_DECAY * old)
                 o_tile[slot] = new.astype(BF16)
                 here, there = out_pair(q, slot)
@@ -304,7 +473,6 @@
             lax.fori_loop(0, num_chunks, row_end, 0)
 
         def drain(i, _):
-            part_copy(i).wait_send()
             both(gram_send_copy, core, i, lambda cp: cp.wait_send())
             both(poly_send_copy, core, i, lambda cp: cp.wait_send())
             return 0
@@ -321,57 +489,70 @@
             w_forward(side, from_core).wait_send()
     w_pair().wait_send()
 
+    def sent(j, _):
+        for side in (0, 1):
+            for h in range(CORES):
+                up_copy(side, h, j).wait_send()
+        mate_copy(j).wait_send()
+        return 0
+    lax.fori_loop(0, pieces, sent, 0)
+
+    def paired(i, _):
+        pair_copy(i).wait_send()
+        return 0
+    lax.fori_loop(0, chips * pieces, paired, 0)
+
 
 def solution(mesh):
     group = mesh.shape['dp']
 
-    def orthogonal_update(direction, sq_norm, weight):
-        slab, num_cols = weight.shape
+    def local_step(grad_part, momentum, weight):
+        slab, num_cols = weight.shape[1:]
         rows = slab * group
         half = num_cols // CORES
         scale = 0.2 * math.sqrt(max(rows, num_cols))
         num_chunks = half // CHUNK
+        chips = group // CORES
+        pieces = slab // PIECE
         anywhere = pl.BlockSpec(memory_space=pl.ANY)
         dma = pltpu.SemaphoreType.DMA
+        shape = jax.ShapeDtypeStruct
 
         def kernel(*refs):
-            newton_schulz(group, rows, half, scale, *refs)
-        shape = jax.ShapeDtypeStruct
-        return pl.pallas_call(
+            muon(group, rows, half, scale, *refs)
+        outs = pl.pallas_call(
             kernel,
-            name='newton_schulz',
-            out_shape=(shape((rows, num_cols), BF16), shape((slab, num_cols), BF16), shape((rows, half), F32)),
+            name='muon',
+            out_shape=(shape((rows, num_cols), BF16), shape((slab, num_cols), BF16), shape((slab, num_cols), F32),
+                       shape((chips, CORES * slab, half), F32), shape((chips, slab, num_cols), F32), shape((3, 2, slab, half), F32)),
             in_specs=[anywhere] * 3,
-            out_specs=(anywhere,) * 3,
+            out_specs=(anywhere,) * 6,
             scratch_shapes=[
                 pltpu.VMEM((num_chunks + 1, rows, CHUNK), BF16),
                 pltpu.VMEM((rows, rows), BF16),
                 pltpu.VMEM((rows, rows), BF16),
                 pltpu.VMEM((5, BLOCK, BLOCK), F32),
                 pltpu.VMEM((5, BLOCK, BLOCK), F32),
-                pltpu.VMEM((2, 1024, CHUNK), F32),
                 pltpu.VMEM((2, 1024, CHUNK), BF16),
+                pltpu.VMEM((6, PIECE, half), F32),
+                pltpu.VMEM((2, DEPTH, PIECE, half), F32),
+                pltpu.VMEM((CORES * num_chunks, slab, CHUNK), BF16),
+                pltpu.VMEM((8, half), F32),
                 pltpu.VMEM((8, 128), F32),
-                dma((num_chunks + 1,)),
+                pltpu.VMEM((group, 8, 128), F32),
+                dma((chips * pieces,)), dma((chips * pieces,)), dma((2, DEPTH)), dma((3, 2, pieces)), dma((6,)),
+                dma((group,)), dma((group,)), dma((2, 2, pieces)), dma((2, 2, pieces)), dma((pieces,)), dma((pieces,)),
+                dma((2, 2, pieces // 2)), dma((2, 2, pieces // 2)),
                 dma((5,)), dma((5,)), dma((5, 2)), dma((5, 2)), dma((5, 2)), dma((5, 2)),
                 dma((2, 2, 2)), dma((2, 2, 2)), dma((2, 2)), dma((2, 2)),
                 dma((5,)),
                 dma((2,)), dma((2,)), dma((2 * num_chunks,)),
                 dma((num_chunks,)), dma((num_chunks,)), dma((num_chunks,)),
             ],
-            compiler_params=pltpu.CompilerParams(collective_id=1, has_side_effects=True, vmem_limit_bytes=60 * 2 ** 20),
-        )(direction, sq_norm, weight)
-
-    def local_step(grad_part, momentum, weight):
-        grad = lax.psum_scatter(grad_part[0], 'dp', scatter_dimension=1, tiled=True) / group
-        new_momentum = MOMENTUM * momentum + grad
-        direction = (grad + MOMENTUM * new_momentum).astype(BF16)
-        as_float = direction.astype(F32)
-        sq_norm = lax.psum(jnp.sum(as_float * as_float), 'dp')
-        whole = lax.all_gather(direction[0], 'dp', axis=0, tiled=True)
-        weight_bf16, ortho, _ = orthogonal_update(whole, jnp.full((8, 128), sq_norm, F32), weight[0])
-        scale = 0.2 * math.sqrt(max(weight_bf16.shape))
+            compiler_params=pltpu.CompilerParams(collective_id=1, has_side_effects=True, vmem_limit_bytes=63 * 2 ** 20),
+        )(grad_part[0, 0], momentum[0], weight[0])
+        weight_bf16, ortho, new_momentum = outs[:3]
         new_weight = weight - LEARN_RATE * (scale * ortho[None].astype(F32) + WEIGHT_DECAY * weight)
-        return new_momentum, new_weight, weight_bf16[None]
+        return new_momentum[None], new_weight, weight_bf16[None]
 
     return jax.shard_map(local_step, mesh=mesh, in_specs=(P(('mp', 'dp')), P('mp', 'dp'), P('mp', 'dp')), out_specs=(P('mp', 'dp'), P('mp', 'dp'), P('mp')), check_vma=False)

time: 823 us -> 740 us (0.90)
  waiting for transfers between devices: 412 us -> 0 us
  Pallas kernels: 343 us -> 707 us
  between operations: 14.1 us -> 0.65 us
  blocking collectives: 13.4 us -> 0 us
  other arithmetic: 18 us -> 8.84 us
    pallas_call x1, Pallas kernels: 343 us -> 707 us  [local_step(): pl.pallas_call(kernel, name='muon', out_shape=(shape((rows, num_cols), BF...]
    reduce_scatter x1 -> x0, waiting for transfers between devices: 290 us -> none  [local_step(): lax.psum_scatter(grad_part[0], 'dp', scatter_dimension=1, tiled=True)]
    all_gather x1 -> x0, waiting for transfers between devices: 122 us -> none  [local_step(): whole = lax.all_gather(direction[0], 'dp', axis=0, tiled=True)]
    psum x1 -> x0, blocking collectives: 13.4 us -> none  [local_step(): sq_norm = lax.psum(jnp.sum(as_float * as_float), 'dp')]
    reduce_sum x1 -> x0, other arithmetic: 9.28 us -> none  [local_step(): sq_norm = lax.psum(jnp.sum(as_float * as_float), 'dp')]
    unnamed x1 -> x4, local copies, waits for them, and re-layouts: 20.1 us -> 23.2 us
  transfers between devices with their start and end apart: 2 -> 0, of which waited for: 2 -> 0; matrix products, arithmetic and copies ran while one was open for 0% -> 0% of each run, Pallas kernels for 0% -> 0%
where the time goes in v2:
time: 740 us
  Pallas kernels  707 us (96%)
  local copies, waits for them, and re-layouts  23.2 us (3%)
  other arithmetic  8.84 us (1%)
    pallas_call x1, Pallas kernels, local_step(): pl.pallas_call(kernel, name='muon', out_shape=(shape((rows, num_cols), BF...  707 us
    unnamed x4, local copies, waits for them, and re-layouts  23.2 us

profile of v2, /device:TPU:113, one launch (start us, length us, event | category | flops | bytes accessed | tf_op | source)
XLA Modules:
  0.0 739.5 jit_solution(3171556920102743615)
XLA Ops:
  0.6 706.8 %muon.1 = (bf16[2048,7168]{1,0:T(8,128)(2,1)}, bf16[256,7168]{1,0:T(8,128)(2,1)}, f32[256,7168]{1,0:T(8,128)}, f32[4,512,3584]{2,1,0:T(8,128)}, f32[4,256,7168]{2,1,0:T(8,128)}, /*index=5*/f32[3,2,256,3584]{3,2,1,0:T(8,128)}) custom-call(f32[2048,7168]{1,0:T(8,128)} %bitcast.11, f32[256,7168]{1,0:T(8,128)} %bitcast.14, f32[256,7168]{1,0:T(8,128)} %bitcast.12), custom_call_target="tpu_custom_call" | custom-call | tf_op jit(solution)/shard_map/muon/pallas_call | solution.py:523
  707.5 0.0 copy-start
  707.5 8.8 %fusion.1 = f32[1,256,7168]{2,1,0:T(8,128)} fusion(f32[1,256,7168]{2,1,0:T(8,128)} %param.5, bf16[256,7168]{1,0:T(8,128)(2,1)} %get-tuple-element.7), kind=kLoop, calls=%fused_computation.2 | loop fusion | flops 11010048 | bytes 18350080 | tf_op jit(solution)/shard_map/sub | solution.py:555
  716.3 0.0 copy-done
  716.3 3.0 copy.8
  719.4 20.1 %copy.9 = bf16[1,2048,7168]{2,1,0:T(8,128)(2,1)} copy(bf16[1,2048,7168]{2,1,0:T(8,128)(2,1)} %bitcast.13) | data formatting | bytes 58720256
Async XLA Ops:
  707.5 8.9 %copy-start = (f32[256,7168]{1,0:T(8,128)S(1)}, f32[256,7168]{1,0:T(8,128)}, u32[]{:S(2)}) copy-start(f32[256,7168]{1,0:T(8,128)} %get-tuple-element.6) | copy-start | bytes 22020100

commit v3 on v2

--- a/solution.py
+++ b/solution.py
@@ -21,7 +21,14 @@
 CHUNK = 512
 PIECE = 32
 DEPTH = 4
-BLOCKS = (((0, 0), (2, 0), (1, 1), (3, 1), (3, 3)), ((1, 0), (3, 0), (2, 1), (2, 2), (3, 2)))
+EARLY = 2
+BLOCKS = (((0, 0), (2, 0), (1, 1), (2, 2), (3, 3)), ((1, 0), (3, 0), (2, 1), (3, 1), (3, 2)))
+SQUARES = (((0, 0), (1, 1), (2, 0), (2, 2), (3, 3)), ((1, 0), (2, 1), (3, 0), (3, 1), (3, 2)))
+
+OWNER = [next((core for core in range(CORES) if (max(r, c), min(r, c)) in BLOCKS[core])) for r in range(4) for c in range(4)]
+PLACE = [BLOCKS[OWNER[r * 4 + c]].index((max(r, c), min(r, c))) for r in range(4) for c in range(4)]
+NEAR_ONE = [0, 0, 1, 0, 1, 2]
+NEAR_TWO = [0, 1, 1, 2, 2, 2]
 
 
 def lookup(index, values):
@@ -31,9 +38,9 @@
     return result
 
 
-def block_of(core, index):
-    row = jnp.where(core == 0, lookup(index, [b[0] for b in BLOCKS[0]]), lookup(index, [b[0] for b in BLOCKS[1]]))
-    col = jnp.where(core == 0, lookup(index, [b[1] for b in BLOCKS[0]]), lookup(index, [b[1] for b in BLOCKS[1]]))
+def block_of(core, index, table=BLOCKS):
+    row = jnp.where(core == 0, lookup(index, [b[0] for b in table[0]]), lookup(index, [b[0] for b in table[1]]))
+    col = jnp.where(core == 0, lookup(index, [b[1] for b in table[0]]), lookup(index, [b[1] for b in table[1]]))
     return row, col
 
 
@@ -42,8 +49,8 @@
 
 
 def muon(group, rows, half, scale, grad_ref, mom_ref, w_ref, wb_ref, xrow_ref, nmom_ref, wcol_ref, pair_ref, arrived_ref,
-         x_ref, gram, poly, part_out, part_in, o_tile, tiles, stage, own, square_acc, sq_out, sq_in,
-         pair_send, pair_recv, rs_send, rs_recv, in_sem, sq_send, sq_recv, up_send, up_recv, mate_send, mate_recv, pass_send, pass_recv,
+         x_ref, gram, poly, parts, part_in, tiles, stage, own, square_acc, sq_out, sq_in,
+         pair_send, pair_recv, rs_send, rs_recv, in_sem, sq_send, sq_recv, up_send, up_recv, mate_send, mate_recv, pass_send, pass_recv, far_send, far_recv, share_send, share_recv,
          part_send, part_recv, gram_send, gram_recv, poly_send, poly_recv,
          w_send, w_recv, w_fwd_send, w_fwd_recv, tile_sem, out_sem, out_send, out_recv, row_sem, row_send, row_recv):
     me = lax.axis_index('dp')
@@ -157,6 +164,12 @@
             def _():
                 stage[side, slot] = tiles[3 * side] + tiles[3 * side + 1]
             rs_copy(q, side).start()
+
+    def send_up(j):
+        for side in (0, 1):
+            for h in range(CORES):
+                up_copy(side, h, j).start()
+        mate_copy(j).start()
 
     def finish(j):
         pair_copy(3 * pieces + j).wait_recv()
@@ -183,10 +196,10 @@
             as_float = update.astype(F32)
             square_acc[...] += jnp.sum((as_float * as_float).reshape(PIECE // 8, 8, half), axis=0)
         nmom_copy(j, 1).wait()
-        for side in (0, 1):
-            for h in range(CORES):
-                up_copy(side, h, j).start()
-        mate_copy(j).start()
+
+        @pl.when(j < pieces // 2)
+        def _():
+            send_up(j)
 
     def reduce_step(q, _):
         @pl.when(q < 3 * pieces)
@@ -210,6 +223,11 @@
         return remote(sq_out, sq_in.at[me], sq_send.at[other], sq_recv.at[other], lax.rem(me + other, group))
     for other in range(1, group):
         sq_copy(other).start()
+
+    def send_rest(j, _):
+        send_up(j)
+        return 0
+    lax.fori_loop(pieces // 2, pieces, send_rest, 0)
     for other in range(1, group):
         sq_copy(other).wait()
     square = sq_in[0, 0:1, 0:1]
@@ -233,10 +251,14 @@
         return 0
     lax.fori_loop(0, pieces, normalise_mate, 0)
 
-    def pass_copy(side, from_core, j):
-        row0 = (side_chip[1 - side] * CORES + from_core) * slab + (side * (pieces // 2) + j) * PIECE
-        where = x_ref.at[pl.ds(0, num_chunks), pl.ds(pl.multiple_of(row0, PIECE), PIECE), :]
-        return remote(where, where, pass_send.at[side, from_core, j], pass_recv.at[side, from_core, j], side_chip[side] * CORES + core)
+    def pass_copy(side, from_core, c):
+        row0 = (side_chip[1 - side] * CORES + from_core) * slab + side * (slab // 2)
+        where = x_ref.at[c, pl.ds(pl.multiple_of(row0, slab // 2), slab // 2), :]
+        return remote(where, where, pass_send.at[side, from_core, c], pass_recv.at[side, from_core, c], side_chip[side] * CORES + core)
+
+    def pass_on(side, c):
+        for from_core in range(CORES):
+            pass_copy(side, from_core, c).start()
 
     def arrive(j, _):
         for side in (0, 1):
@@ -244,11 +266,11 @@
                 up_copy(side, core, j, from_core).wait_recv()
                 normalise((side_chip[1 - side] * CORES + from_core) * slab + j * PIECE, PIECE)
 
-                @pl.when(j // (pieces // 2) == side)
-                def _():
-                    pass_copy(side, from_core, j - side * (pieces // 2)).start()
-        return 0
-    lax.fori_loop(0, pieces, arrive, 0)
+            @pl.when(j == (side + 1) * (pieces // 2) - 1)
+            def _():
+                for c in range(EARLY):
+                    pass_on(side, c)
+        return 0
 
     piece = slab // 2
 
@@ -268,49 +290,171 @@
     def w_own():
         return pltpu.make_async_copy(w_ref.at[:, pl.ds(pl.multiple_of(core * half, half), half)],
                                      wcol_ref.at[chip, pl.ds(pl.multiple_of(core * slab, slab), slab), :], tile_sem.at[2])
+    def slot_of(c, t):
+        return lax.rem(c + 2 * slots - t, slots)
+
+    def gram_copy(b, index, row, col):
+        where = gram.at[span(row, BLOCK), span(col, BLOCK)]
+        return remote(where, where, gram_send.at[index, b], gram_recv.at[index, b], partner)
+
+    def poly_copy(b, index, row, col):
+        where = poly.at[span(row, BLOCK), span(col, BLOCK)]
+        return remote(where, where, poly_send.at[index, b], poly_recv.at[index, b], partner)
+
+    def both(copy, owner, index, act, table=BLOCKS):
+        row, col = block_of(owner, index, table)
+
+        @pl.when(row != col)
+        def _():
+            act(copy(1, index, col, row))
+        act(copy(0, index, row, col))
+
+    def start(copy):
+        copy.start()
+
+    def arrived(copy):
+        copy.wait_recv()
+
+    def left(copy):
+        copy.wait_send()
+
+    def part_copy(index):
+        return remote(parts.at[index], part_in.at[index], part_send.at[index], part_recv.at[index], partner)
+
+    def gram_value(t, row, col):
+        ri, rj = span(row, BLOCK), span(col, BLOCK)
+        xi = jnp.concatenate([x_ref[slot_of(c, t), ri, :] for c in range(num_chunks)], axis=1)
+        xj = jnp.concatenate([x_ref[slot_of(c, t), rj, :] for c in range(num_chunks)], axis=1)
+        return lax.dot_general(xi, xj, (((1,), (1,)), ((), ())), preferred_element_type=F32)
+
+    def finish_gram(index, value):
+        row, col = block_of(core, index)
+        block = (value + part_in[index]).astype(BF16)
+        gram[span(row, BLOCK), span(col, BLOCK)] = block
+        gram[span(col, BLOCK), span(row, BLOCK)] = block.T
+
+    def near_chip(order):
+        return jnp.where(order == 0, chip, jnp.where(order == 1, side_chip[0], side_chip[1]))
+
+    def near_block(index):
+        one = near_chip(lookup(index, NEAR_ONE))
+        two = near_chip(lookup(index, NEAR_TWO))
+        row, col = jnp.maximum(one, two), jnp.minimum(one, two)
+        cell = row * chips + col
+        return row, col, lookup(cell, PLACE), lookup(cell, OWNER) == core
+
+    def near_gram(index, _):
+        row, col, place, mine = near_block(index)
+        parts[jnp.where(mine, 5 + place, place)] = gram_value(0, row, col)
+
+        @pl.when(jnp.logical_not(mine))
+        def _():
+            part_copy(place).start()
+        return 0
+
+    def near_finish(index, _):
+        row, col, place, mine = near_block(index)
+
+        @pl.when(mine)
+        def _():
+            part_copy(place).wait_recv()
+            finish_gram(place, parts[5 + place])
+            both(gram_copy, core, place, start)
+        return 0
+
+    def near_meet(index, _):
+        row, col, place, mine = near_block(index)
+
+        @pl.when(mine)
+        def _():
+            both(gram_copy, core, place, left)
+
+        @pl.when(jnp.logical_not(mine))
+        def _():
+            part_copy(place).wait_send()
+            both(gram_copy, 1 - core, place, arrived)
+        return 0
+
+    def far_block(chip_index, core_index, side):
+        right, behind = lax.rem(chip_index + 1, chips), lax.rem(chip_index + chips - 1, chips)
+        if side == 1:
+            one, two = jnp.where(core_index == 0, chip_index, behind), right
+        else:
+            one, two = jnp.where(core_index == 0, chip_index, behind), behind
+        return jnp.maximum(one, two), jnp.minimum(one, two)
+
+    def far_copy(side):
+        row, col = far_block(chip, core, side)
+        where = gram.at[span(row, BLOCK), span(col, BLOCK)]
+        return remote(where, where, far_send.at[side], far_recv.at[side], side_chip[side] * CORES + core)
+
+    def share_copy(side, owner, b):
+        row, col = far_block(side_chip[1 - side], owner, side)
+        if b == 1:
+            row, col = col, row
+        where = gram.at[span(row, BLOCK), span(col, BLOCK)]
+        return remote(where, where, share_send.at[side, b], share_recv.at[side, b], partner)
+
+    def share(side, owner, act):
+        act(share_copy(side, owner, 0))
+        row, col = far_block(side_chip[1 - side], owner, side)
+
+        @pl.when(row != col)
+        def _():
+            act(share_copy(side, owner, 1))
+
+    near_gram(0, 0)
+    lax.fori_loop(0, pieces, arrive, 0)
+    lax.fori_loop(1, 6, near_gram, 0)
+    lax.fori_loop(0, 6, near_finish, 0)
+    lax.fori_loop(0, 6, near_meet, 0)
+    for side in (0, 1):
+        far_copy(side).start()
+    for c in range(EARLY, num_chunks):
+        for side in (0, 1):
+            pass_on(side, c)
     for part in (0, 1):
         for side in (0, 1):
             for h in range(CORES):
                 w_first(side, h, part if side == 0 else 1 - part).start()
     w_pair().start()
     w_own().start()
-
-    def late(j, _):
+    for side in (0, 1):
+        far_copy(side).wait_recv()
+        row, col = far_block(side_chip[1 - side], core, side)
+        turned = gram[span(row, BLOCK), span(col, BLOCK)].T
+
+        @pl.when(row != col)
+        def _():
+            gram[span(col, BLOCK), span(row, BLOCK)] = turned
+        share(side, core, start)
+    for side in (0, 1):
+        share(side, 1 - core, arrived)
+        far_copy(side).wait_send()
+        share(side, core, left)
+
+    def sent(j, _):
         for side in (0, 1):
-            for from_core in range(CORES):
-                pass_copy(side, from_core, j).wait()
-        return 0
-    lax.fori_loop(0, pieces // 2, late, 0)
-
-    def slot_of(c, t):
-        return lax.rem(c + 2 * slots - t, slots)
-
-    def gram_send_copy(b, index, row, col):
-        return remote(gram.at[span(row, BLOCK), span(col, BLOCK)], gram.at[span(row, BLOCK), span(col, BLOCK)],
-                      gram_send.at[index, b], gram_recv.at[index, b], partner)
-
-    def poly_send_copy(b, index, row, col):
-        return remote(poly.at[span(row, BLOCK), span(col, BLOCK)], poly.at[span(row, BLOCK), span(col, BLOCK)],
-                      poly_send.at[index, b], poly_recv.at[index, b], partner)
-
-    def both(copy, owner, index, act):
-        row, col = block_of(owner, index)
-        act(copy(0, index, row, col))
-
-        @pl.when(row != col)
-        def _():
-            act(copy(1, index, col, row))
-
-    def part_copy(index):
-        return remote(part_out.at[index], part_in.at[index], part_send.at[index], part_recv.at[index], partner)
+            for h in range(CORES):
+                up_copy(side, h, j).wait_send()
+        mate_copy(j).wait_send()
+        return 0
+    lax.fori_loop(0, pieces, sent, 0)
+
+    tall = 1024
+    per_tall = tall // slab
+
+    def apply_value(q, t):
+        c, m = q // 2, lax.rem(q, 2)
+        rm = span(m, tall)
+        src = slot_of(c, t)
+        total = jnp.dot(poly[rm, :], x_ref[src], preferred_element_type=F32)
+        return (COEF_A * x_ref[src, rm, :].astype(F32) + total).astype(BF16)
+
+    def keep(q, t, value):
+        x_ref[slot_of(q // 2, t + 1), span(lax.rem(q, 2), tall), :] = value
 
     def step(t, _):
-        def gram_block(row, col):
-            ri, rj = span(row, BLOCK), span(col, BLOCK)
-            xi = jnp.concatenate([x_ref[slot_of(c, t), ri, :] for c in range(num_chunks)], axis=1)
-            xj = jnp.concatenate([x_ref[slot_of(c, t), rj, :] for c in range(num_chunks)], axis=1)
-            return lax.dot_general(xi, xj, (((1,), (1,)), ((), ())), preferred_element_type=F32)
-
         @pl.when(t == 2)
         def _():
             for side in (0, 1):
@@ -318,83 +462,55 @@
                     w_first(side, 0, side, from_core).wait_recv()
                     w_forward(side, from_core).start()
 
-        def gram_step(index, _):
-            owner = jnp.where(index < 5, 1 - core, core)
-            place = lax.rem(index, 5)
-            row, col = block_of(owner, place)
-            value = gram_block(row, col)
-
-            @pl.when(index < 5)
-            def _():
-                part_out[place] = value
-                part_copy(place).start()
-
-            @pl.when(index >= 5)
-            def _():
-                part_copy(place).wait_recv()
-                block = (value + part_in[place]).astype(BF16)
-                gram[span(row, BLOCK), span(col, BLOCK)] = block
-
-                @pl.when(row != col)
-                def _():
-                    gram[span(col, BLOCK), span(row, BLOCK)] = block.T
-                both(gram_send_copy, core, place, lambda cp: cp.start())
+        @pl.when(t > 0)
+        def _():
+            def gram_other(index, _):
+                row, col = block_of(1 - core, index)
+                parts[index] = gram_value(t, row, col)
+                part_copy(index).start()
+                return 0
+            lax.fori_loop(0, 5, gram_other, 0)
+
+            def gram_own(index, _):
+                part_copy(index).wait_recv()
+                row, col = block_of(core, index)
+                finish_gram(index, gram_value(t, row, col))
+                both(gram_copy, core, index, start)
+                return 0
+            lax.fori_loop(0, 5, gram_own, 0)
+
+        def square(index, _):
+            @pl.when((index == 0) & (t > 0))
+            def _():
+                for i in range(3):
+                    both(gram_copy, 1 - core, i, arrived)
+
+            @pl.when((index == 1) & (t > 0))
+            def _():
+                both(gram_copy, 1 - core, 3, arrived)
+
+            @pl.when((index == 2) & (t > 0))
+            def _():
+                both(gram_copy, 1 - core, 4, arrived)
+            row, col = block_of(core, index, SQUARES)
+            ri, rj = span(row, BLOCK), span(col, BLOCK)
+            value = jnp.dot(gram[ri, :], gram[:, rj], preferred_element_type=F32)
+            block = (COEF_B * gram[ri, rj].astype(F32) + COEF_C * value).astype(BF16)
+            poly[ri, rj] = block
+            poly[rj, ri] = block.T
+            both(poly_copy, core, index, start, SQUARES)
             return 0
-        lax.fori_loop(0, 10, gram_step, 0)
-
-        def poly_step(index, _):
-            @pl.when(index == 0)
-            def _():
-                for i in range(4):
-                    both(gram_send_copy, 1 - core, i, lambda cp: cp.wait_recv())
-
-            @pl.when(index == 1)
-            def _():
-                both(gram_send_copy, 1 - core, 4, lambda cp: cp.wait_recv())
-            row, col = block_of(core, index)
-            ri, rj = span(row, BLOCK), span(col, BLOCK)
-            square = jnp.dot(gram[ri, :], gram[:, rj], preferred_element_type=F32)
-            block = (COEF_B * gram[ri, rj].astype(F32) + COEF_C * square).astype(BF16)
-            poly[ri, rj] = block
-
-            @pl.when(row != col)
-            def _():
-                poly[rj, ri] = block.T
-            both(poly_send_copy, core, index, lambda cp: cp.start())
-            return 0
-        lax.fori_loop(0, 5, poly_step, 0)
-
-        def part_drain(i, _):
+        lax.fori_loop(0, 5, square, 0)
+
+        def part_drain(i, carry):
             part_copy(i).wait_send()
-            return 0
-        lax.fori_loop(0, 5, part_drain, 0)
-        tall = 1024
-
-        def poly_waits(q):
-            @pl.when(q == 0)
-            def _():
-                for i in range(4):
-                    both(poly_send_copy, 1 - core, i, lambda cp: cp.wait_recv())
-
-            @pl.when(q == 1)
-            def _():
-                both(poly_send_copy, 1 - core, 4, lambda cp: cp.wait_recv())
-
-        def apply_block(q):
+            return carry
+        pl.when(t > 0)(lambda: lax.fori_loop(0, 5, part_drain, None))
+
+        def tile_load(q):
             c, m = q // 2, lax.rem(q, 2)
-            rm = span(m, tall)
-            src, dst = slot_of(c, t), slot_of(c, t + 1)
-            total = jnp.dot(poly[rm, :], x_ref[src], preferred_element_type=F32)
-            return c, m, rm, dst, (COEF_A * x_ref[src, rm, :].astype(F32) + total).astype(BF16)
-
-        @pl.when(t < NS_STEPS - 1)
-        def _():
-            def apply_step(q, _):
-                poly_waits(q)
-                c, m, rm, dst, value = apply_block(q)
-                x_ref[dst, rm, :] = value
-                return 0
-            lax.fori_loop(0, 2 * num_chunks, apply_step, 0)
+            slot = lax.rem(q, 2)
+            return pltpu.make_async_copy(wcol_ref.at[pl.ds(2 * m, 2), :, span(c, CHUNK)], parts.at[pl.ds(2 * slot, 2)], tile_sem.at[slot])
 
         @pl.when(t == NS_STEPS - 1)
         def _():
@@ -404,16 +520,52 @@
                     w_forward(side, from_core).wait_recv()
             w_pair().wait_recv()
             w_own().wait()
-
-            def tile_load(q):
+            tile_load(0).start()
+            tile_load(1).start()
+
+        def poly_ready(q):
+            @pl.when(q == 0)
+            def _():
+                for index in range(4):
+                    both(poly_copy, 1 - core, index, arrived, SQUARES)
+
+            @pl.when(q == 1)
+            def _():
+                both(poly_copy, 1 - core, 4, arrived, SQUARES)
+
+        def far_ready(c):
+            @pl.when(t == 0)
+            def _():
+                for side in (0, 1):
+                    for from_core in range(CORES):
+                        pass_copy(side, from_core, c).wait()
+
+        @pl.when(t < NS_STEPS - 1)
+        def _():
+            def apply_half(q, _):
+                pl.when(q == 0)(lambda: far_ready(0))
+                poly_ready(q)
+                keep(q, t, apply_value(q, t))
+                return 0
+            lax.fori_loop(0, 2, apply_half, 0)
+
+            def apply_chunk(c, _):
+                far_ready(c)
+                src = slot_of(c, t)
+                total = jnp.dot(poly[...], x_ref[src], preferred_element_type=F32)
+                x_ref[slot_of(c, t + 1)] = (COEF_A * x_ref[src].astype(F32) + total).astype(BF16)
+                return 0
+            lax.fori_loop(1, num_chunks, apply_chunk, 0)
+
+        @pl.when(t == NS_STEPS - 1)
+        def _():
+            def out_pair(q):
                 c, m = q // 2, lax.rem(q, 2)
-                return pltpu.make_async_copy(wcol_ref.at[pl.ds(2 * m, 2), :, span(c, CHUNK)], part_out.at[pl.ds(2 * lax.rem(q, 2), 2)], tile_sem.at[lax.rem(q, 2)])
-
-            def out_pair(q, slot):
-                c, m = q // 2, lax.rem(q, 2)
-                where = wb_ref.at[span(m, tall), pl.ds(pl.multiple_of(core * half + c * CHUNK, CHUNK), CHUNK)]
-                return (pltpu.make_async_copy(o_tile.at[slot], where, out_sem.at[slot]),
-                        remote(o_tile.at[slot], where, out_send.at[slot], out_recv.at[q], partner))
+                slot = lax.rem(q, 2)
+                where = wb_ref.at[pl.ds(m * per_tall, per_tall), :, pl.ds(pl.multiple_of(core * half + c * CHUNK, CHUNK), CHUNK)]
+                tile = own.at[pl.ds(slot * per_tall, per_tall)]
+                return (pltpu.make_async_copy(tile, where, out_sem.at[slot]),
+                        remote(tile, where, out_send.at[slot], out_recv.at[q], partner))
 
             def row_pair(c):
                 slot = slot_of(c, t + 1)
@@ -421,47 +573,58 @@
                 return (pltpu.make_async_copy(x_ref.at[slot, span(me, slab), :], xrow_ref.at[:, cols], row_sem.at[c]),
                         remote(x_ref.at[slot, span(partner, slab), :], xrow_ref.at[:, cols], row_send.at[c], row_recv.at[c], partner))
 
-            tile_load(0).start()
-
-            def last_step(q, _):
-                poly_waits(q)
-
-                @pl.when(q + 1 < 2 * num_chunks)
-                def _():
-                    tile_load(q + 1).start()
-                c, m, rm, dst, value = apply_block(q)
-                x_ref[dst, rm, :] = value
-                slot = lax.rem(q, 2)
+            def out_ready(q):
                 tile_load(q).wait()
 
                 @pl.when(q >= 2)
                 def _():
-                    here, there = out_pair(q - 2, slot)
+                    here, there = out_pair(q - 2)
                     here.wait()
                     there.wait_send()
-                old = part_out[pl.ds(2 * slot, 2)].reshape(tall, CHUNK)
-                new = old - LEARN_RATE * (scale * value.astype(F32) + WEIGHT_DECAY * old)
-                o_tile[slot] = new.astype(BF16)
-                here, there = out_pair(q, slot)
+
+            def new_weight(q):
+                c, m = q // 2, lax.rem(q, 2)
+                slot = lax.rem(q, 2)
+                old = parts[pl.ds(2 * slot, 2)].reshape(tall, CHUNK)
+                ortho = x_ref[slot_of(c, t + 1), span(m, tall), :].astype(F32)
+                new = ((1.0 - LEARN_RATE * WEIGHT_DECAY) * old - (LEARN_RATE * scale) * ortho).astype(BF16)
+                own[pl.ds(slot * per_tall, per_tall)] = new.reshape(per_tall, slab, CHUNK)
+
+            def out_start(q):
+                here, there = out_pair(q)
                 here.start()
                 there.start()
 
-                @pl.when(m == 1)
+            def last_step(q, _):
+                if NS_STEPS == 1:
+                    pl.when(lax.rem(q, 2) == 0)(lambda: far_ready(q // 2))
+                poly_ready(q)
+                keep(q, t, apply_value(q, t))
+                out_ready(q)
+                new_weight(q)
+                out_start(q)
+
+                @pl.when(q + 2 < 2 * num_chunks)
                 def _():
-                    here, there = row_pair(c)
+                    tile_load(q + 2).start()
+
+                @pl.when(lax.rem(q, 2) == 1)
+                def _():
+                    here, there = row_pair(q // 2)
                     here.start()
                     there.start()
                 return 0
-            lax.fori_loop(0, 2 * num_chunks, last_step, 0)
-            for q in (2 * num_chunks - 2, 2 * num_chunks - 1):
-                here, there = out_pair(q, q % 2)
+            last = 2 * num_chunks - 1
+            lax.fori_loop(0, last + 1, last_step, 0)
+            for q in (last - 1, last):
+                here, there = out_pair(q)
                 here.wait()
                 there.wait_send()
 
             def out_arrival(q, _):
                 c, m = q // 2, lax.rem(q, 2)
-                where = wb_ref.at[span(m, tall), pl.ds(pl.multiple_of((1 - core) * half + c * CHUNK, CHUNK), CHUNK)]
-                remote(o_tile.at[0], where, out_send.at[0], out_recv.at[q], partner).wait_recv()
+                where = wb_ref.at[pl.ds(m * per_tall, per_tall), :, pl.ds(pl.multiple_of((1 - core) * half + c * CHUNK, CHUNK), CHUNK)]
+                remote(own.at[pl.ds(0, per_tall)], where, out_send.at[0], out_recv.at[q], partner).wait_recv()
                 return 0
             lax.fori_loop(0, 2 * num_chunks, out_arrival, 0)
 
@@ -473,8 +636,10 @@
             lax.fori_loop(0, num_chunks, row_end, 0)
 
         def drain(i, _):
-            both(gram_send_copy, core, i, lambda cp: cp.wait_send())
-            both(poly_send_copy, core, i, lambda cp: cp.wait_send())
+            @pl.when(t > 0)
+            def _():
+                both(gram_copy, core, i, left)
+            both(poly_copy, core, i, left, SQUARES)
             return 0
         lax.fori_loop(0, 5, drain, 0)
         return 0
@@ -488,14 +653,6 @@
         for from_core in range(CORES):
             w_forward(side, from_core).wait_send()
     w_pair().wait_send()
-
-    def sent(j, _):
-        for side in (0, 1):
-            for h in range(CORES):
-                up_copy(side, h, j).wait_send()
-        mate_copy(j).wait_send()
-        return 0
-    lax.fori_loop(0, pieces, sent, 0)
 
     def paired(i, _):
         pair_copy(i).wait_send()
@@ -523,7 +680,7 @@
         outs = pl.pallas_call(
             kernel,
             name='muon',
-            out_shape=(shape((rows, num_cols), BF16), shape((slab, num_cols), BF16), shape((slab, num_cols), F32),
+            out_shape=(shape((group, slab, num_cols), BF16), shape((slab, num_cols), BF16), shape((slab, num_cols), F32),
                        shape((chips, CORES * slab, half), F32), shape((chips, slab, num_cols), F32), shape((3, 2, slab, half), F32)),
             in_specs=[anywhere] * 3,
             out_specs=(anywhere,) * 6,
@@ -531,9 +688,8 @@
                 pltpu.VMEM((num_chunks + 1, rows, CHUNK), BF16),
                 pltpu.VMEM((rows, rows), BF16),
                 pltpu.VMEM((rows, rows), BF16),
+                pltpu.VMEM((10, BLOCK, BLOCK), F32),
                 pltpu.VMEM((5, BLOCK, BLOCK), F32),
-                pltpu.VMEM((5, BLOCK, BLOCK), F32),
-                pltpu.VMEM((2, 1024, CHUNK), BF16),
                 pltpu.VMEM((6, PIECE, half), F32),
                 pltpu.VMEM((2, DEPTH, PIECE, half), F32),
                 pltpu.VMEM((CORES * num_chunks, slab, CHUNK), BF16),
@@ -542,17 +698,17 @@
                 pltpu.VMEM((group, 8, 128), F32),
                 dma((chips * pieces,)), dma((chips * pieces,)), dma((2, DEPTH)), dma((3, 2, pieces)), dma((6,)),
                 dma((group,)), dma((group,)), dma((2, 2, pieces)), dma((2, 2, pieces)), dma((pieces,)), dma((pieces,)),
-                dma((2, 2, pieces // 2)), dma((2, 2, pieces // 2)),
+                dma((2, 2, num_chunks)), dma((2, 2, num_chunks)), dma((2,)), dma((2,)), dma((2, 2)), dma((2, 2)),
                 dma((5,)), dma((5,)), dma((5, 2)), dma((5, 2)), dma((5, 2)), dma((5, 2)),
                 dma((2, 2, 2)), dma((2, 2, 2)), dma((2, 2)), dma((2, 2)),
                 dma((5,)),
                 dma((2,)), dma((2,)), dma((2 * num_chunks,)),
                 dma((num_chunks,)), dma((num_chunks,)), dma((num_chunks,)),
             ],
-            compiler_params=pltpu.CompilerParams(collective_id=1, has_side_effects=True, vmem_limit_bytes=63 * 2 ** 20),
+            compiler_params=pltpu.CompilerParams(collective_id=1, has_side_effects=True, vmem_limit_bytes=67043328),
         )(grad_part[0, 0], momentum[0], weight[0])
         weight_bf16, ortho, new_momentum = outs[:3]
         new_weight = weight - LEARN_RATE * (scale * ortho[None].astype(F32) + WEIGHT_DECAY * weight)
-        return new_momentum[None], new_weight, weight_bf16[None]
+        return new_momentum[None], new_weight, weight_bf16.reshape(1, rows, num_cols)
 
     return jax.shard_map(local_step, mesh=mesh, in_specs=(P(('mp', 'dp')), P('mp', 'dp'), P('mp', 'dp')), out_specs=(P('mp', 'dp'), P('mp', 'dp'), P('mp')), check_vma=False)

time: 740 us -> 697 us (0.942)
  Pallas kernels: 707 us -> 664 us
    pallas_call x1, Pallas kernels: 707 us -> 664 us  [local_step(): pl.pallas_call(kernel, name='muon', out_shape=(shape((group, slab, num_co...]
where the time goes in v3:
time: 697 us
  Pallas kernels  664 us (95%)
  local copies, waits for them, and re-layouts  23.2 us (3%)
  other arithmetic  8.84 us (1%)
    pallas_call x1, Pallas kernels, local_step(): pl.pallas_call(kernel, name='muon', out_shape=(shape((group, slab, num_co...  664 us
    unnamed x4, local copies, waits for them, and re-layouts  23.2 us

profile of v3, /device:TPU:113, one launch (start us, length us, event | category | flops | bytes accessed | tf_op | source)
XLA Modules:
  0.0 696.6 jit_solution(12648902840768845855)
XLA Ops:
  0.6 663.9 %muon.1 = (bf16[8,256,7168]{2,1,0:T(8,128)(2,1)}, bf16[256,7168]{1,0:T(8,128)(2,1)}, f32[256,7168]{1,0:T(8,128)}, f32[4,512,3584]{2,1,0:T(8,128)}, f32[4,256,7168]{2,1,0:T(8,128)}, /*index=5*/f32[3,2,256,3584]{3,2,1,0:T(8,128)}) custom-call(f32[2048,7168]{1,0:T(8,128)} %bitcast.11, f32[256,7168]{1,0:T(8,128)} %bitcast.14, f32[256,7168]{1,0:T(8,128)} %bitcast.12), custom_call_target="tpu_custom_call" | custom-call | tf_op jit(solution)/shard_map/muon/pallas_call | solution.py:680
  664.6 0.0 copy-start
  664.6 8.8 %fusion.1 = f32[1,256,7168]{2,1,0:T(8,128)} fusion(f32[1,256,7168]{2,1,0:T(8,128)} %param.5, bf16[256,7168]{1,0:T(8,128)(2,1)} %get-tuple-element.7), kind=kLoop, calls=%fused_computation.2 | loop fusion | flops 11010048 | bytes 18350080 | tf_op jit(solution)/shard_map/sub | solution.py:711
  673.4 0.0 copy-done
  673.4 3.0 copy.8
  676.5 20.1 %copy.9 = bf16[1,2048,7168]{2,1,0:T(8,128)(2,1)} copy(bf16[1,2048,7168]{2,1,0:T(8,128)(2,1)} %bitcast.13) | data formatting | bytes 58720256
Async XLA Ops:
  664.6 8.9 %copy-start = (f32[256,7168]{1,0:T(8,128)S(1)}, f32[256,7168]{1,0:T(8,128)}, u32[]{:S(2)}) copy-start(f32[256,7168]{1,0:T(8,128)} %get-tuple-element.6) | copy-start | bytes 22020100

commit v4 on v3

v4 whole, which is shorter than its diff:
```python
import math
import jax
import jax.numpy as jnp
from jax import lax
from jax.experimental import pallas as pl
from jax.experimental.pallas import tpu as pltpu
from jax.sharding import PartitionSpec as P

MOMENTUM = 0.95
LEARN_RATE = 2.0
WEIGHT_DECAY = 0.25
NS_STEPS = 5
COEF_A = 3.4445
COEF_B = -4.7750
COEF_C = 2.0315

MESH = pl.DeviceIdType.MESH
F32, BF16 = jnp.float32, jnp.bfloat16
CORES = 2
BLOCK = 512
CHUNK = 512
DEPTH = 4
EAGER = 4
EARLY = 1
W_EARLY = 5
OTHERS = ((0, 1), (2, 3, 4))
BLOCKS = (((0, 0), (2, 1), (3, 1), (2, 0), (3, 3)), ((1, 1), (1, 0), (3, 0), (3, 2), (2, 2)))
SQUARES = (((0, 0), (3, 0), (3, 1), (3, 2), (3, 3)), ((1, 1), (1, 0), (2, 0), (2, 1), (2, 2)))
NEAR = (((0, 2), (0, 1), (0, 0)), ((2, 2), (1, 2), (1, 1)))


def block_of(core, index, table=BLOCKS):
    def pick(owner, i):
        values = [block[i] for block in table[owner]]
        if isinstance(index, int):
            return values[index]
        result = jnp.int32(values[0])
        for place, value in enumerate(values[1:], 1):
            result = jnp.where(index == place, jnp.int32(value), result)
        return result
    return tuple(jnp.where(core == 0, pick(0, i), pick(1, i)) for i in range(2))


def diagonal(index):
    return isinstance(index, int) and index in (0, 4)


def span(index, size):
    return pl.ds(pl.multiple_of(index * size, size), size)


def muon(group, rows, half, scale, grad_ref, mom_ref, w_ref, wb_ref, xrow_ref, nmom_ref, wcol_ref, pair_ref, arrived_ref,
         x_ref, gram, poly, parts, part_in, square_acc, sq_out, sq_in,
         pair_send, pair_recv, rs_send, rs_recv, in_sem, sq_send, sq_recv, up_send, up_recv, mate_send, mate_recv, pass_send, pass_recv, far_send, far_recv, share_send, share_recv,
         part_send, part_recv, gram_send, gram_recv, poly_send, poly_recv,
         w_send, w_recv, w_fwd_send, w_fwd_recv, w_mate_send, w_mate_recv, w_own_sem, tile_sem, out_sem, out_send, out_recv, row_sem, row_send, row_recv):
    me = lax.axis_index('dp')
    core, chip = lax.rem(me, CORES), me // CORES
    chips = group // CORES
    slab = rows // group
    partner = chip * CORES + (1 - core)
    side_chip = (lax.rem(chip + 1, chips), lax.rem(chip + chips - 1, chips))
    far_chip = lax.rem(chip + 2, chips)
    num_chunks = half // CHUNK
    slots = num_chunks + 1

    def remote(src, dst, send, recv, device):
        return pltpu.make_async_remote_copy(src, dst, send, recv, device_id={'dp': device}, device_id_type=MESH)

    barrier = pltpu.get_barrier_semaphore()
    for other in range(1, group):
        pl.semaphore_signal(barrier, inc=1, device_id={'dp': lax.rem(me + other, group)}, device_id_type=MESH)
    pl.semaphore_wait(barrier, group - 1)

    def tile(index):
        return parts.at[index // 2, pl.ds(pl.multiple_of(lax.rem(index, 2) * slab, slab), slab), :]

    def staged(side, slot):
        return tile(6 + side * DEPTH + slot)

    def own(index):
        return poly.at[span(index // 4, slab), span(lax.rem(index, 4), CHUNK)]

    def dest_chip(order):
        return jnp.where(order == 0, far_chip, jnp.where(order == 1, side_chip[0], jnp.where(order == 2, side_chip[1], chip)))

    def rows_of(device):
        return span(device, slab)

    def columns(which, j):
        return pl.ds(pl.multiple_of(which * half + j * CHUNK, CHUNK), CHUNK)

    def pair_copy(order, j, which):
        i = (order * num_chunks + j) * 2 + which
        return remote(grad_ref.at[rows_of(dest_chip(order) * CORES + 1 - core), columns(which, j)], pair_ref.at[order, :, columns(which, j)],
                      pair_send.at[i], pair_recv.at[i], partner)

    def pair_start(i, _):
        order, j = i // num_chunks, lax.rem(i, num_chunks)
        for which in (0, 1):
            pair_copy(order, j, which).start()
        return 0
    lax.fori_loop(0, chips * num_chunks, pair_start, 0)

    def grad_loads(order, j, which, base):
        return (pltpu.make_async_copy(grad_ref.at[rows_of(dest_chip(order) * CORES + core), columns(which, j)], tile(base), in_sem.at[base]),
                pltpu.make_async_copy(pair_ref.at[order, :, columns(which, j)], tile(base + 1), in_sem.at[base + 1]))

    def arrived_load(phase, side, j, base):
        return pltpu.make_async_copy(arrived_ref.at[phase, side, j], tile(base), in_sem.at[base])

    def rs_copy(q, side):
        phase, j = q // num_chunks, lax.rem(q, num_chunks)
        slot = lax.rem(q, DEPTH)
        return remote(staged(side, slot), arrived_ref.at[phase, side, j],
                      rs_send.at[side, slot], rs_recv.at[phase, side, j], side_chip[side] * CORES + core)

    def up_copy(side, h, j, sender=None):
        return remote(own(h * num_chunks + j), x_ref.at[j, rows_of(me), :],
                      up_send.at[side, h, j], up_recv.at[side, core if sender is None else sender, j], side_chip[side] * CORES + h)

    def mate_copy(j):
        return remote(own((1 - core) * num_chunks + j), x_ref.at[j, rows_of(me), :], mate_send.at[j], mate_recv.at[j], partner)

    def nmom_copy(j, which):
        return pltpu.make_async_copy(tile(5), nmom_ref.at[:, columns(which, j)], in_sem.at[5])

    square_acc[...] = jnp.zeros_like(square_acc)

    def send_sums(q):
        phase, j = q // num_chunks, lax.rem(q, num_chunks)
        slot = lax.rem(q, DEPTH)
        for side in (0, 1):
            order = jnp.where(phase == 0, 0, 1 + side)
            which = jnp.where(phase == 1, 1 - side, side)
            pair_copy(order, j, which).wait_recv()
            for load in grad_loads(order, j, which, 3 * side):
                load.start()

            @pl.when(phase == 2)
            def _():
                rs_copy(j, side).wait_recv()
                arrived_load(0, side, j, 3 * side + 2).start()

        for side in (0, 1):
            order = jnp.where(phase == 0, 0, 1 + side)
            which = jnp.where(phase == 1, 1 - side, side)

            @pl.when(q >= DEPTH)
            def _():
                rs_copy(q - DEPTH, side).wait_send()
            for load in grad_loads(order, j, which, 3 * side):
                load.wait()

            @pl.when(phase == 2)
            def _():
                arrived_load(0, side, j, 3 * side + 2).wait()
                staged(side, slot)[...] = (tile(3 * side)[...] + tile(3 * side + 1)[...]) + tile(3 * side + 2)[...]

            @pl.when(phase != 2)
            def _():
                staged(side, slot)[...] = tile(3 * side)[...] + tile(3 * side + 1)[...]
            rs_copy(q, side).start()

    def send_up(j):
        for side in (0, 1):
            for h in range(CORES):
                up_copy(side, h, j).start()
        mate_copy(j).start()

    def finish(j):
        for which in (0, 1):
            pair_copy(3, j, which).wait_recv()
            loads = list(grad_loads(3, j, which, 0))
            for side in (0, 1):
                phase = 2 if side == which else 1
                rs_copy(phase * num_chunks + j, side).wait_recv()
                loads.append(arrived_load(phase, side, j, 2 + side))
            loads.append(pltpu.make_async_copy(mom_ref.at[:, columns(which, j)], tile(4), in_sem.at[4]))
            for load in loads:
                load.start()
            for load in loads:
                load.wait()
            if which == 1:
                nmom_copy(j, 0).wait()
            mean = (((tile(0)[...] + tile(1)[...]) + tile(2)[...]) + tile(3)[...]) / group
            momentum = MOMENTUM * tile(4)[...] + mean
            tile(5)[...] = momentum
            nmom_copy(j, which).start()
            update = (mean + MOMENTUM * momentum).astype(BF16)
            own(which * num_chunks + j)[...] = update
            as_float = update.astype(F32)
            square_acc[...] += jnp.sum((as_float * as_float).reshape(slab // 8, 8, CHUNK), axis=0)
        nmom_copy(j, 1).wait()

        @pl.when(j < EAGER)
        def _():
            send_up(j)

    def reduce_step(q, _):
        @pl.when(q < 3 * num_chunks)
        def _():
            send_sums(q)

        @pl.when(q >= 2 * num_chunks + DEPTH)
        def _():
            finish(q - 2 * num_chunks - DEPTH)
        return 0
    lax.fori_loop(0, 3 * num_chunks + DEPTH, reduce_step, 0)
    for side in (0, 1):
        for last in range(DEPTH):
            rs_copy(3 * num_chunks - DEPTH + last, side).wait_send()

    total = jnp.sum(square_acc[...])
    sq_out[...] = jnp.full(sq_out.shape, total, F32)
    sq_in[me] = jnp.full(sq_out.shape, total, F32)

    def sq_copy(other):
        return remote(sq_out, sq_in.at[me], sq_send.at[other], sq_recv.at[other], lax.rem(me + other, group))
    for other in range(1, group):
        sq_copy(other).start()

    def send_rest(j, _):
        send_up(j)
        return 0
    lax.fori_loop(EAGER, num_chunks, send_rest, 0)
    for other in range(1, group):
        sq_copy(other).wait()
    square = sq_in[0, 0:1, 0:1]
    for i in range(1, group):
        square = square + sq_in[i, 0:1, 0:1]
    inverse = 1.0 / (jnp.sqrt(square) + 1e-7)

    def normalise(j, row0, size):
        r = pl.ds(pl.multiple_of(row0, slab), size)
        x_ref[j, r, :] = (x_ref[j, r, :].astype(F32) * inverse).astype(BF16)

    def pass_copy(side, c):
        where = x_ref.at[c, rows_of(side_chip[1 - side] * CORES + side), :]
        return remote(where, where, pass_send.at[side, c], pass_recv.at[side, c], side_chip[side] * CORES + core)

    def w_first(side, h, c, sender=None):
        return remote(w_ref.at[:, columns(h, c)], wcol_ref.at[c, chip, span(core, slab), :],
                      w_send.at[side, h, c], w_recv.at[side, core if sender is None else sender, c], side_chip[side] * CORES + h)

    def w_forward(side, c):
        where = wcol_ref.at[c, side_chip[1 - side], pl.ds(side * slab, slab), :]
        return remote(where, where, w_fwd_send.at[side, c], w_fwd_recv.at[side, c], side_chip[side] * CORES + core)

    def w_pair(c):
        return remote(w_ref.at[:, columns(1 - core, c)], wcol_ref.at[c, chip, span(core, slab), :], w_mate_send.at[c], w_mate_recv.at[c], partner)

    def w_own(c):
        return pltpu.make_async_copy(w_ref.at[:, columns(core, c)], wcol_ref.at[c, chip, span(core, slab), :], w_own_sem.at[c])

    def w_pass(c):
        for side in (0, 1):
            w_first(side, 0, c, side).wait_recv()
            w_forward(side, c).start()

    def w_ready(c):
        for side in (0, 1):
            w_first(side, 0, c, 1 - side).wait_recv()
            w_forward(side, c).wait_recv()
        w_pair(c).wait_recv()
        w_own(c).wait()

    def slot_of(c, t):
        return lax.rem(c + 2 * slots - t, slots)

    def gram_copy(b, index, row, col):
        where = gram.at[span(row, BLOCK), span(col, BLOCK)]
        return remote(where, where, gram_send.at[index, b], gram_recv.at[index, b], partner)

    def poly_copy(b, index, row, col):
        where = poly.at[span(row, BLOCK), span(col, BLOCK)]
        return remote(where, where, poly_send.at[index, b], poly_recv.at[index, b], partner)

    def both(copy, owner, index, act, table=BLOCKS):
        row, col = block_of(owner, index, table)
        if not diagonal(index):
            act(copy(1, index, col, row))
        act(copy(0, index, row, col))

    def start(copy):
        copy.start()

    def arrived(copy):
        copy.wait_recv()

    def left(copy):
        copy.wait_send()

    def part_copy(index):
        return remote(parts.at[index], part_in.at[index], part_send.at[index], part_recv.at[index], partner)

    small = BLOCK // 2
    ROWS_ROWS = (((1,), (1,)), ((), ()))

    def product(rows_at, index, row, col):
        if diagonal(index):
            left = lax.dot_general(rows_at(row, 0, BLOCK), rows_at(row, 0, small), ROWS_ROWS, preferred_element_type=F32)
            corner = lax.dot_general(rows_at(row, small, small), rows_at(row, small, small), ROWS_ROWS, preferred_element_type=F32)
            return left, corner
        return (lax.dot_general(rows_at(row, 0, BLOCK), rows_at(col, 0, BLOCK), ROWS_ROWS, preferred_element_type=F32),)

    def pieces_of(ref, value):
        if len(value) == 2:
            return (ref[:, 0:small], ref[small:, small:])
        return (ref[...],)

    def put_block(ref, row, col, value):
        if len(value) == 2:
            at = ref.at[span(row, BLOCK), span(row, BLOCK)]
            left, corner = (v.astype(BF16) for v in value)
            at[:, 0:small] = left
            at[small:, small:] = corner
            at[0:small, small:] = left[small:].T
        else:
            block = value[0].astype(BF16)
            ref[span(row, BLOCK), span(col, BLOCK)] = block
            ref[span(col, BLOCK), span(row, BLOCK)] = block.T

    def x_rows(t):
        def rows_at(block, offset, size):
            r = pl.ds(pl.multiple_of(block * BLOCK + offset, small), size)
            return jnp.concatenate([x_ref[slot_of(c, t), r, :] for c in range(num_chunks)], axis=1)
        return rows_at

    def gram_rows(block, offset, size):
        return gram[pl.ds(pl.multiple_of(block * BLOCK + offset, small), size), :]

    def near_chip(order):
        return (chip, side_chip[0], side_chip[1])[order]

    def near_block(one, two):
        one, two = near_chip(one), near_chip(two)
        return jnp.maximum(one, two), jnp.minimum(one, two)

    def near_owned(owner, place):
        rows_cols = [(near_block(*NEAR[c][place])) for c in range(CORES)]
        return tuple(jnp.where(owner == 0, rows_cols[0][i], rows_cols[1][i]) for i in range(2))

    def near_sum(j, place):
        row, col = near_owned(jnp.where(place < 3, 1 - core, core), place % 3)
        value = lax.dot_general(x_ref[j, span(row, BLOCK), :], x_ref[j, span(col, BLOCK), :], (((1,), (1,)), ((), ())), preferred_element_type=F32)
        slot = place % 3 + 5 * (place // 3)

        @pl.when(j == 0)
        def _():
            parts[slot] = value

        @pl.when(j > 0)
        def _():
            parts[slot] = parts[slot] + value

    def near_copy(place, b):
        row, col = near_owned(core, place)
        if b == 1:
            row, col = col, row
        where = gram.at[span(row, BLOCK), span(col, BLOCK)]
        return remote(where, where, gram_send.at[place, b], gram_recv.at[place, b], partner)

    def near_both(place, act):
        act(near_copy(place, 0))
        row, col = near_owned(core, place)

        @pl.when(row != col)
        def _():
            act(near_copy(place, 1))

    def near_arrived(place):
        near_copy(place, 0).wait_recv()
        row, col = near_owned(1 - core, place)

        @pl.when(row != col)
        def _():
            near_copy(place, 1).wait_recv()

    def arrive(j, _):
        x_ref[j, rows_of(me), :] = (own(core * num_chunks + j)[...].astype(F32) * inverse).astype(BF16)
        mate_copy(j).wait_recv()
        normalise(j, partner * slab, slab)
        for side in (0, 1):
            for from_core in range(CORES):
                up_copy(side, core, j, from_core).wait_recv()
            normalise(j, side_chip[1 - side] * CORES * slab, CORES * slab)
        for place in range(6):
            near_sum(j, place)
        return 0

    def far_block(chip_index, core_index, side):
        right, behind = lax.rem(chip_index + 1, chips), lax.rem(chip_index + chips - 1, chips)
        if side == 1:
            one, two = jnp.where(core_index == 0, chip_index, behind), right
        else:
            one, two = jnp.where(core_index == 0, chip_index, behind), behind
        return jnp.maximum(one, two), jnp.minimum(one, two)

    def far_copy(side):
        row, col = far_block(chip, core, side)
        where = gram.at[span(row, BLOCK), span(col, BLOCK)]
        return remote(where, where, far_send.at[side], far_recv.at[side], side_chip[side] * CORES + core)

    def share_copy(side, owner, b):
        row, col = far_block(side_chip[1 - side], owner, side)
        if b == 1:
            row, col = col, row
        where = gram.at[span(row, BLOCK), span(col, BLOCK)]
        return remote(where, where, share_send.at[side, b], share_recv.at[side, b], partner)

    def share(side, owner, act):
        act(share_copy(side, owner, 0))
        row, col = far_block(side_chip[1 - side], owner, side)

        @pl.when(row != col)
        def _():
            act(share_copy(side, owner, 1))

    lax.fori_loop(0, num_chunks, arrive, 0)

    def sent(j, _):
        for side in (0, 1):
            for h in range(CORES):
                up_copy(side, h, j).wait_send()
        mate_copy(j).wait_send()
        return 0
    lax.fori_loop(0, num_chunks, sent, 0)

    for place in range(3):
        part_copy(place).start()

    for c in range(EARLY):
        for side in (0, 1):
            pass_copy(side, c).start()
    for place in range(3):
        part_copy(place).wait_recv()
        row, col = near_owned(core, place)
        block = (parts[5 + place] + part_in[place]).astype(BF16)
        gram[span(row, BLOCK), span(col, BLOCK)] = block
        if place < 2:
            far_copy(place).start()

        @pl.when(row != col)
        def _():
            gram[span(col, BLOCK), span(row, BLOCK)] = block.T
        near_both(place, start)
    for c in range(EARLY, num_chunks):
        for side in (0, 1):
            pass_copy(side, c).start()

    def w_start(c, _):
        for h in range(CORES):
            for side in (0, 1):
                w_first(side, h, c).start()
        w_pair(c).start()
        w_own(c).start()
        return 0
    lax.fori_loop(0, num_chunks, w_start, 0)
    for place in range(3):
        near_arrived(place)
    for side in (0, 1):
        far_copy(side).wait_recv()
        row, col = far_block(side_chip[1 - side], core, side)
        turned = gram[span(row, BLOCK), span(col, BLOCK)].T

        @pl.when(row != col)
        def _():
            gram[span(col, BLOCK), span(row, BLOCK)] = turned
        share(side, core, start)
    for side in (0, 1):
        share(side, 1 - core, arrived)
        far_copy(side).wait_send()
        share(side, core, left)
    for place in range(3):
        near_both(place, left)
        part_copy(place).wait_send()

    tall = 1024

    def apply_value(q, t):
        c, m = q // 2, lax.rem(q, 2)
        rm = span(m, tall)
        src = slot_of(c, t)
        total = jnp.dot(poly[rm, :], x_ref[src], preferred_element_type=F32)
        return (COEF_A * x_ref[src, rm, :].astype(F32) + total).astype(BF16)

    def keep(q, t, value):
        x_ref[slot_of(q // 2, t + 1), span(lax.rem(q, 2), tall), :] = value

    def step(t, _):
        def pass_weights(low, high):
            @pl.when(t == NS_STEPS - 2)
            def _():
                def one(c, _):
                    w_pass(c)
                    return 0
                lax.fori_loop(low, high, one, 0)
        pass_weights(0, W_EARLY)

        @pl.when(t > 0)
        def _():
            for group_of in OTHERS:
                for index in group_of:
                    row, col = block_of(1 - core, index)
                    value = product(x_rows(t), index, row, col)
                    if len(value) == 2:
                        parts[index, :, 0:small] = value[0]
                        parts[index, small:, small:] = value[1]
                    else:
                        parts[index] = value[0]
                for index in group_of:
                    part_copy(index).start()

            def gram_own(*indices):
                for index in indices:
                    part_copy(index).wait_recv()
                for index in indices:
                    row, col = block_of(core, index)
                    value = product(x_rows(t), index, row, col)
                    put_block(gram, row, col, tuple(v + w for v, w in zip(value, pieces_of(part_in.at[index], value))))
                for index in indices:
                    both(gram_copy, core, index, start)

            def gram_middle(index, _):
                gram_own(index)
                return 0
            gram_own(0, 1)
            lax.fori_loop(2, 4, gram_middle, 0)
            gram_own(4)

        def squares(indices, needs):
            @pl.when(t > 0)
            def _():
                for index in needs:
                    both(gram_copy, 1 - core, index, arrived)
            for index in indices:
                row, col = block_of(core, index, SQUARES)
                value = product(gram_rows, index, row, col)
                old = pieces_of(gram.at[span(row, BLOCK), span(col, BLOCK)], value)
                put_block(poly, row, col, tuple(COEF_B * g.astype(F32) + COEF_C * v for g, v in zip(old, value)))
            for index in indices:
                both(poly_copy, core, index, start, SQUARES)
        squares((0,), (0, 1, 2))
        squares((1,), (3,))
        squares((2,), ())
        squares((3,), (4,))
        squares((4,), ())

        def part_drain(i, carry):
            part_copy(i).wait_send()
            return carry
        pl.when(t > 0)(lambda: lax.fori_loop(0, 5, part_drain, None))

        def tile_load(q):
            c, m = q // 2, lax.rem(q, 2)
            slot = lax.rem(q, 2)
            return pltpu.make_async_copy(wcol_ref.at[c, pl.ds(2 * m, 2)], parts.at[pl.ds(2 * slot, 2)], tile_sem.at[slot])

        @pl.when(t == NS_STEPS - 1)
        def _():
            w_ready(0)
            if NS_STEPS > 1:
                for index in range(5):
                    both(gram_copy, core, index, left)
            tile_load(0).start()
            tile_load(1).start()

        def poly_ready(indices):
            for index in indices:
                both(poly_copy, 1 - core, index, arrived, SQUARES)

        def far_ready(c):
            @pl.when(t == 0)
            def _():
                for side in (0, 1):
                    pass_copy(side, c).wait()

        def apply_rows(c, low, high):
            src = slot_of(c, t)
            total = jnp.dot(poly[low:high, :], x_ref[src], preferred_element_type=F32)
            x_ref[slot_of(c, t + 1), low:high, :] = (COEF_A * x_ref[src, low:high, :].astype(F32) + total).astype(BF16)
        far_ready(0)
        poly_ready((0, 1, 2))
        apply_rows(0, 0, BLOCK)
        pass_weights(W_EARLY, num_chunks)
        poly_ready((3, 4))
        apply_rows(0, BLOCK, rows)

        @pl.when(t < NS_STEPS - 1)
        def _():
            def apply_chunk(c, _):
                far_ready(c)
                apply_rows(c, 0, rows)
                return 0
            lax.fori_loop(1, num_chunks, apply_chunk, 0)

        @pl.when(t == NS_STEPS - 1)
        def _():
            def out_pair(q):
                c, m = q // 2, lax.rem(q, 2)
                slot = lax.rem(q, 2)
                where = wb_ref.at[span(m, tall), columns(core, c)]
                new = gram.at[span(slot, tall), 0:CHUNK]
                return (pltpu.make_async_copy(new, where, out_sem.at[slot]),
                        remote(new, where, out_send.at[slot], out_recv.at[q], partner))

            def row_pair(c):
                slot = slot_of(c, t + 1)
                cols = pl.ds(pl.multiple_of(core * half + c * CHUNK, CHUNK), CHUNK)
                return (pltpu.make_async_copy(x_ref.at[slot, span(me, slab), :], xrow_ref.at[:, cols], row_sem.at[c]),
                        remote(x_ref.at[slot, span(partner, slab), :], xrow_ref.at[:, cols], row_send.at[c], row_recv.at[c], partner))

            def out_ready(q):
                tile_load(q).wait()

                @pl.when(q >= 2)
                def _():
                    here, there = out_pair(q - 2)
                    here.wait()
                    there.wait_send()

            def new_weight(q):
                c, m = q // 2, lax.rem(q, 2)
                slot = lax.rem(q, 2)
                old = parts[pl.ds(2 * slot, 2)].reshape(tall, CHUNK)
                ortho = x_ref[slot_of(c, t + 1), span(m, tall), :].astype(F32)
                new = ((1.0 - LEARN_RATE * WEIGHT_DECAY) * old - (LEARN_RATE * scale) * ortho).astype(BF16)
                gram[span(slot, tall), 0:CHUNK] = new

            def out_start(q):
                here, there = out_pair(q)
                here.start()
                there.start()

            def last_step(q, _):
                if NS_STEPS == 1:
                    pl.when(lax.rem(q, 2) == 0)(lambda: far_ready(q // 2))
                keep(q, t, apply_value(q, t))
                out_ready(q)
                new_weight(q)
                out_start(q)

                @pl.when(q + 2 < 2 * num_chunks)
                def _():
                    pl.when(lax.rem(q, 2) == 0)(lambda: w_ready(q // 2 + 1))
                    tile_load(q + 2).start()

                @pl.when(lax.rem(q, 2) == 1)
                def _():
                    here, there = row_pair(q // 2)
                    here.start()
                    there.start()
                return 0
            last = 2 * num_chunks - 1
            for q in (0, 1):
                out_ready(q)
                new_weight(q)
                out_start(q)
                if q == 0:
                    w_ready(1)
                tile_load(q + 2).start()
            for copy in row_pair(0):
                copy.start()
            lax.fori_loop(2, last + 1, last_step, 0)
            for q in (last - 1, last):
                here, there = out_pair(q)
                here.wait()
                there.wait_send()

            def out_arrival(q, _):
                c, m = q // 2, lax.rem(q, 2)
                where = wb_ref.at[span(m, tall), columns(1 - core, c)]
                remote(gram.at[0:tall, 0:CHUNK], where, out_send.at[0], out_recv.at[q], partner).wait_recv()
                return 0
            lax.fori_loop(0, 2 * num_chunks, out_arrival, 0)

            def row_end(c, _):
                here, there = row_pair(c)
                here.wait()
                there.wait()
                return 0
            lax.fori_loop(0, num_chunks, row_end, 0)

        for index in range(5):
            @pl.when((t > 0) & (t < NS_STEPS - 1))
            def _():
                both(gram_copy, core, index, left)
            both(poly_copy, core, index, left, SQUARES)
        return 0
    lax.fori_loop(0, NS_STEPS, step, 0)

    def w_end(c, _):
        for side in (0, 1):
            for h in range(CORES):
                w_first(side, h, c).wait_send()
            w_forward(side, c).wait_send()
        w_pair(c).wait_send()
        return 0
    lax.fori_loop(0, num_chunks, w_end, 0)

    def paired(i, _):
        order, j = i // num_chunks, lax.rem(i, num_chunks)
        for which in (0, 1):
            pair_copy(order, j, which).wait_send()
        return 0
    lax.fori_loop(0, chips * num_chunks, paired, 0)


def hand_over(decay, step, wide_ref, nmom_ref, xrow_ref, w_ref, wide_out, nmom_out, weight_out, wide, nmom, xrow, weight, load_sem, store_sem):
    count = wide.shape[0]
    loads = [pltpu.make_async_copy(w_ref, weight, load_sem.at[count]), pltpu.make_async_copy(xrow_ref, xrow, load_sem.at[count + 1])]
    loads += [pltpu.make_async_copy(nmom_ref, nmom, load_sem.at[count + 2])]
    loads += [pltpu.make_async_copy(wide_ref.at[i], wide.at[i], load_sem.at[i]) for i in range(count)]
    stores = [pltpu.make_async_copy(weight, weight_out, store_sem.at[count]), pltpu.make_async_copy(nmom, nmom_out, store_sem.at[count + 2])]
    stores += [pltpu.make_async_copy(wide.at[i], wide_out.at[i], store_sem.at[i]) for i in range(count)]
    for load in loads:
        load.start()
    loads[0].wait()
    loads[1].wait()

    def rows_of(i, _):
        r = span(i, 16)
        weight[r, :] = decay * weight[r, :] - step * xrow[r, :].astype(F32)
        return 0
    lax.fori_loop(0, weight.shape[0] // 16, rows_of, 0)
    stores[0].start()
    for load, store in zip(loads[2:], stores[1:]):
        load.wait()
        store.start()
    for store in stores:
        store.wait()


def solution(mesh):
    group = mesh.shape['dp']

    def local_step(grad_part, momentum, weight):
        slab, num_cols = weight.shape[1:]
        rows = slab * group
        half = num_cols // CORES
        scale = 0.2 * math.sqrt(max(rows, num_cols))
        num_chunks = half // CHUNK
        chips = group // CORES
        anywhere = pl.BlockSpec(memory_space=pl.ANY)
        dma = pltpu.SemaphoreType.DMA
        shape = jax.ShapeDtypeStruct

        def kernel(*refs):
            muon(group, rows, half, scale, *refs)
        outs = pl.pallas_call(
            kernel,
            name='muon',
            out_shape=(shape((rows, num_cols), BF16), shape((slab, num_cols), BF16), shape((slab, num_cols), F32),
                       shape((num_chunks, chips, CORES * slab, CHUNK), F32), shape((chips, slab, num_cols), F32), shape((3, 2, num_chunks, slab, CHUNK), F32)),
            in_specs=[anywhere] * 3,
            out_specs=(anywhere,) * 6,
            scratch_shapes=[
                pltpu.VMEM((num_chunks + 1, rows, CHUNK), BF16),
                pltpu.VMEM((rows, rows), BF16),
                pltpu.VMEM((rows, rows), BF16),
                pltpu.VMEM((10, BLOCK, BLOCK), F32),
                pltpu.VMEM((5, BLOCK, BLOCK), F32),
                pltpu.VMEM((8, CHUNK), F32),
                pltpu.VMEM((8, 128), F32),
                pltpu.VMEM((group, 8, 128), F32),
                dma((chips * num_chunks * 2,)), dma((chips * num_chunks * 2,)), dma((2, DEPTH)), dma((3, 2, num_chunks)), dma((6,)),
                dma((group,)), dma((group,)), dma((2, 2, num_chunks)), dma((2, 2, num_chunks)), dma((num_chunks,)), dma((num_chunks,)),
                dma((2, num_chunks)), dma((2, num_chunks)), dma((2,)), dma((2,)), dma((2, 2)), dma((2, 2)),
                dma((5,)), dma((5,)), dma((5, 2)), dma((5, 2)), dma((5, 2)), dma((5, 2)),
                dma((2, 2, num_chunks)), dma((2, 2, num_chunks)), dma((2, num_chunks)), dma((2, num_chunks)),
                dma((num_chunks,)), dma((num_chunks,)), dma((num_chunks,)), dma((2,)),
                dma((2,)), dma((2,)), dma((2 * num_chunks,)),
                dma((num_chunks,)), dma((num_chunks,)), dma((num_chunks,)),
            ],
            compiler_params=pltpu.CompilerParams(collective_id=1, has_side_effects=True, vmem_limit_bytes=67043328),
        )(grad_part[0, 0], momentum[0], weight[0])
        weight_bf16, ortho, new_momentum = outs[:3]

        def last_kernel(*refs):
            hand_over(1.0 - LEARN_RATE * WEIGHT_DECAY, LEARN_RATE * scale, *refs)
        weight_bf16, new_momentum, new_weight = pl.pallas_call(
            last_kernel,
            name='hand_over',
            out_shape=(shape((group, slab, num_cols), BF16), shape((slab, num_cols), F32), shape((slab, num_cols), F32)),
            in_specs=[anywhere] * 4,
            out_specs=(anywhere,) * 3,
            scratch_shapes=[
                pltpu.VMEM((group, slab, num_cols), BF16),
                pltpu.VMEM((slab, num_cols), F32),
                pltpu.VMEM((slab, num_cols), BF16),
                pltpu.VMEM((slab, num_cols), F32),
                dma((group + 3,)), dma((group + 3,)),
            ],
            compiler_params=pltpu.CompilerParams(vmem_limit_bytes=56 * 2 ** 20),
        )(weight_bf16.reshape(group, slab, num_cols), new_momentum, ortho, weight[0])
        return new_momentum[None], new_weight[None], weight_bf16.reshape(1, rows, num_cols)

    return jax.shard_map(local_step, mesh=mesh, in_specs=(P(('mp', 'dp')), P('mp', 'dp'), P('mp', 'dp')), out_specs=(P('mp', 'dp'), P('mp', 'dp'), P('mp')), check_vma=False)
```

time: 697 us -> 675 us (0.968)
  local copies, waits for them, and re-layouts: 23.2 us -> 0 us
  Pallas kernels: 664 us -> 673 us
  other arithmetic: 8.84 us -> 0 us
    unnamed x4 -> x0, local copies, waits for them, and re-layouts: 23.2 us -> none
    pallas_call x1 -> x2, Pallas kernels: 664 us -> 673 us  [the longest x1 644 us: local_step(): pl.pallas_call(kernel, name='muon', out_shape=(shape((rows, num_cols), BF...]
    sub x1 -> x0, other arithmetic: 8.84 us -> none  [local_step(): weight - LEARN_RATE * (scale * ortho[None].astype(F32) + WEIGHT_DECAY * w...]
where the time goes in v4:
time: 675 us; the launch traced here: 674 us
  Pallas kernels  673 us (100%)
    pallas_call x1, Pallas kernels, local_step(): pl.pallas_call(kernel, name='muon', out_shape=(shape((rows, num_cols), BF...  644 us
    pallas_call x1, Pallas kernels, local_step(): pl.pallas_call(last_kernel, name='hand_over', out_shape=(shape((group, sl...  29.6 us

profile of v4, /device:TPU:113, one launch (start us, length us, event | category | flops | bytes accessed | tf_op | source)
XLA Modules:
  0.0 673.9 jit_solution(12482232552666323317)
XLA Ops:
  0.6 643.5 %muon.1 = (bf16[2048,7168]{1,0:T(8,128)(2,1)}, bf16[256,7168]{1,0:T(8,128)(2,1)}, f32[256,7168]{1,0:T(8,128)}, f32[7,4,512,512]{3,2,1,0:T(8,128)}, f32[4,256,716...) custom-call(f32[2048,7168]{1,0:T(8,128)} %bitcast.7, f32[256,7168]{1,0:T(8,128)} %bitcast.11, f32[256,7168]{1,0:T(8,128)} %bitcast.8), custom_call_target="tpu_custom_call" | custom-call | tf_op jit(solution)/shard_map/muon/pallas_call | solution.py:751
  644.2 29.6 %hand_over.1 = (bf16[8,256,7168]{2,1,0:T(8,128)(2,1)}, f32[256,7168]{1,0:T(8,128)}, f32[256,7168]{1,0:T(8,128)}) custom-call(bf16[8,256,7168]{2,1,0:T(8,128)(2,1)} %bitcast.10, f32[256,7168]{1,0:T(8,128)} %get-tuple-element.10.refs_1_, bf16[256,7168]{1,0:T(8,128)(2,1)} %get-tuple-element.11.refs_2_, f32[256,7168]{1,0:T(8,128)} %bitcast.9), custom_call_target="tpu_custom_call" | custom-call | tf_op jit(solution)/shard_map/hand_over/pallas_call | solution.py:782

commit v5 on v4

--- a/solution.py
+++ b/solution.py
@@ -20,6 +20,8 @@
 BLOCK = 512
 CHUNK = 512
 DEPTH = 4
+KEPT = 4
+VMEM_ROOM = 67 * 2 ** 18
 EAGER = 4
 EARLY = 1
 W_EARLY = 5
@@ -49,11 +51,11 @@
     return pl.ds(pl.multiple_of(index * size, size), size)
 
 
-def muon(group, rows, half, scale, grad_ref, mom_ref, w_ref, wb_ref, xrow_ref, nmom_ref, wcol_ref, pair_ref, arrived_ref,
-         x_ref, gram, poly, parts, part_in, square_acc, sq_out, sq_in,
-         pair_send, pair_recv, rs_send, rs_recv, in_sem, sq_send, sq_recv, up_send, up_recv, mate_send, mate_recv, pass_send, pass_recv, far_send, far_recv, share_send, share_recv,
-         part_send, part_recv, gram_send, gram_recv, poly_send, poly_recv,
-         w_send, w_recv, w_fwd_send, w_fwd_recv, w_mate_send, w_mate_recv, w_own_sem, tile_sem, out_sem, out_send, out_recv, row_sem, row_send, row_recv):
+def muon(group, rows, half, scale, grad_ref, mom_ref, w_ref, x_ref, gram, parts, nmom_ref, wide_ref, rest_ref, wcol_ref, pair_ref, arrived_ref,
+         poly, square_acc, sq_out, sq_in,
+         pair_send, pair_recv, rs_send, rs_recv, in_sem, sq_send, sq_recv, up_send, up_recv, mate_send, mate_recv, pass_send, pass_recv,
+         far_send, far_recv, share_send, share_recv, part_send, part_recv, gram_send, gram_recv, poly_send, poly_recv,
+         w_send, w_recv, w_fwd_send, w_fwd_recv, w_mate_send, w_mate_recv, w_own_sem, tile_sem, out_send, out_recv, row_send, row_recv):
     me = lax.axis_index('dp')
     core, chip = lax.rem(me, CORES), me // CORES
     chips = group // CORES
@@ -121,9 +123,6 @@
 
     def mate_copy(j):
         return remote(own((1 - core) * num_chunks + j), x_ref.at[j, rows_of(me), :], mate_send.at[j], mate_recv.at[j], partner)
-
-    def nmom_copy(j, which):
-        return pltpu.make_async_copy(tile(5), nmom_ref.at[:, columns(which, j)], in_sem.at[5])
 
     square_acc[...] = jnp.zeros_like(square_acc)
 
@@ -181,18 +180,13 @@
                 load.start()
             for load in loads:
                 load.wait()
-            if which == 1:
-                nmom_copy(j, 0).wait()
             mean = (((tile(0)[...] + tile(1)[...]) + tile(2)[...]) + tile(3)[...]) / group
             momentum = MOMENTUM * tile(4)[...] + mean
-            tile(5)[...] = momentum
-            nmom_copy(j, which).start()
+            nmom_ref[which * num_chunks + j] = momentum
             update = (mean + MOMENTUM * momentum).astype(BF16)
             own(which * num_chunks + j)[...] = update
             as_float = update.astype(F32)
             square_acc[...] += jnp.sum((as_float * as_float).reshape(slab // 8, 8, CHUNK), axis=0)
-        nmom_copy(j, 1).wait()
-
         @pl.when(j < EAGER)
         def _():
             send_up(j)
@@ -292,17 +286,18 @@
         copy.wait_send()
 
     def part_copy(index):
-        return remote(parts.at[index], part_in.at[index], part_send.at[index], part_recv.at[index], partner)
+        return remote(parts.at[index], parts.at[5 + index], part_send.at[index], part_recv.at[index], partner)
 
     small = BLOCK // 2
     ROWS_ROWS = (((1,), (1,)), ((), ()))
 
     def product(rows_at, index, row, col):
+        def rows_rows(left, right):
+            terms = [lax.dot_general(a, b, ROWS_ROWS, preferred_element_type=F32) for a, b in zip(rows_at(*left), rows_at(*right))]
+            return sum(terms[1:], terms[0])
         if diagonal(index):
-            left = lax.dot_general(rows_at(row, 0, BLOCK), rows_at(row, 0, small), ROWS_ROWS, preferred_element_type=F32)
-            corner = lax.dot_general(rows_at(row, small, small), rows_at(row, small, small), ROWS_ROWS, preferred_element_type=F32)
-            return left, corner
-        return (lax.dot_general(rows_at(row, 0, BLOCK), rows_at(col, 0, BLOCK), ROWS_ROWS, preferred_element_type=F32),)
+            return rows_rows((row, 0, BLOCK), (row, 0, small)), rows_rows((row, small, small), (row, small, small))
+        return (rows_rows((row, 0, BLOCK), (col, 0, BLOCK)),)
 
     def pieces_of(ref, value):
         if len(value) == 2:
@@ -324,11 +319,11 @@
     def x_rows(t):
         def rows_at(block, offset, size):
             r = pl.ds(pl.multiple_of(block * BLOCK + offset, small), size)
-            return jnp.concatenate([x_ref[slot_of(c, t), r, :] for c in range(num_chunks)], axis=1)
+            return (x_ref[slot_of(c, t), r, :] for c in range(num_chunks))
         return rows_at
 
     def gram_rows(block, offset, size):
-        return gram[pl.ds(pl.multiple_of(block * BLOCK + offset, small), size), :]
+        return (gram[pl.ds(pl.multiple_of(block * BLOCK + offset, small), size), :],)
 
     def near_chip(order):
         return (chip, side_chip[0], side_chip[1])[order]
@@ -344,7 +339,7 @@
     def near_sum(j, place):
         row, col = near_owned(jnp.where(place < 3, 1 - core, core), place % 3)
         value = lax.dot_general(x_ref[j, span(row, BLOCK), :], x_ref[j, span(col, BLOCK), :], (((1,), (1,)), ((), ())), preferred_element_type=F32)
-        slot = place % 3 + 5 * (place // 3)
+        slot = place % 3 + 8 * (place // 3)
 
         @pl.when(j == 0)
         def _():
@@ -436,7 +431,7 @@
     for place in range(3):
         part_copy(place).wait_recv()
         row, col = near_owned(core, place)
-        block = (parts[5 + place] + part_in[place]).astype(BF16)
+        block = (parts[8 + place] + parts[5 + place]).astype(BF16)
         gram[span(row, BLOCK), span(col, BLOCK)] = block
         if place < 2:
             far_copy(place).start()
@@ -477,16 +472,7 @@
         part_copy(place).wait_send()
 
     tall = 1024
-
-    def apply_value(q, t):
-        c, m = q // 2, lax.rem(q, 2)
-        rm = span(m, tall)
-        src = slot_of(c, t)
-        total = jnp.dot(poly[rm, :], x_ref[src], preferred_element_type=F32)
-        return (COEF_A * x_ref[src, rm, :].astype(F32) + total).astype(BF16)
-
-    def keep(q, t, value):
-        x_ref[slot_of(q // 2, t + 1), span(lax.rem(q, 2), tall), :] = value
+    decay, step_size = 1.0 - LEARN_RATE * WEIGHT_DECAY, LEARN_RATE * scale
 
     def step(t, _):
         def pass_weights(low, high):
@@ -498,36 +484,46 @@
                 lax.fori_loop(low, high, one, 0)
         pass_weights(0, W_EARLY)
 
+        def gram_other(*indices):
+            for index in indices:
+                row, col = block_of(1 - core, index)
+                value = product(x_rows(t), index, row, col)
+                if len(value) == 2:
+                    parts[index, :, 0:small] = value[0]
+                    parts[index, small:, small:] = value[1]
+                else:
+                    parts[index] = value[0]
+            for index in indices:
+                part_copy(index).start()
+
+        def gram_own(*indices):
+            for index in indices:
+                part_copy(index).wait_recv()
+            for index in indices:
+                row, col = block_of(core, index)
+                value = product(x_rows(t), index, row, col)
+                put_block(gram, row, col, tuple(v + w for v, w in zip(value, pieces_of(parts.at[5 + index], value))))
+            for index in indices:
+                both(gram_copy, core, index, start)
+
+        def gram_middle(index, _):
+            gram_own(index)
+            return 0
+        later = jnp.minimum(t, 1)
+
+        def alone(act, *indices):
+            def once(_, carry):
+                act(*indices)
+                return carry
+            lax.fori_loop(0, later, once, None)
+        for group_of in OTHERS:
+            alone(gram_other, *group_of)
+        alone(gram_own, 0, 1)
+
         @pl.when(t > 0)
         def _():
-            for group_of in OTHERS:
-                for index in group_of:
-                    row, col = block_of(1 - core, index)
-                    value = product(x_rows(t), index, row, col)
-                    if len(value) == 2:
-                        parts[index, :, 0:small] = value[0]
-                        parts[index, small:, small:] = value[1]
-                    else:
-                        parts[index] = value[0]
-                for index in group_of:
-                    part_copy(index).start()
-
-            def gram_own(*indices):
-                for index in indices:
-                    part_copy(index).wait_recv()
-                for index in indices:
-                    row, col = block_of(core, index)
-                    value = product(x_rows(t), index, row, col)
-                    put_block(gram, row, col, tuple(v + w for v, w in zip(value, pieces_of(part_in.at[index], value))))
-                for index in indices:
-                    both(gram_copy, core, index, start)
-
-            def gram_middle(index, _):
-                gram_own(index)
-                return 0
-            gram_own(0, 1)
             lax.fori_loop(2, 4, gram_middle, 0)
-            gram_own(4)
+        alone(gram_own, 4)
 
         def squares(indices, needs):
             @pl.when(t > 0)
@@ -541,16 +537,21 @@
                 put_block(poly, row, col, tuple(COEF_B * g.astype(F32) + COEF_C * v for g, v in zip(old, value)))
             for index in indices:
                 both(poly_copy, core, index, start, SQUARES)
+        def part_drain(i, carry):
+            part_copy(i).wait_send()
+            return carry
+        pl.when(t > 0)(lambda: lax.fori_loop(0, 5, part_drain, None))
+
         squares((0,), (0, 1, 2))
         squares((1,), (3,))
         squares((2,), ())
         squares((3,), (4,))
+
+        @pl.when((t == NS_STEPS - 1) & (t > 0))
+        def _():
+            for index in range(5):
+                both(gram_copy, core, index, left)
         squares((4,), ())
-
-        def part_drain(i, carry):
-            part_copy(i).wait_send()
-            return carry
-        pl.when(t > 0)(lambda: lax.fori_loop(0, 5, part_drain, None))
 
         def tile_load(q):
             c, m = q // 2, lax.rem(q, 2)
@@ -560,9 +561,6 @@
         @pl.when(t == NS_STEPS - 1)
         def _():
             w_ready(0)
-            if NS_STEPS > 1:
-                for index in range(5):
-                    both(gram_copy, core, index, left)
             tile_load(0).start()
             tile_load(1).start()
 
@@ -576,111 +574,104 @@
                 for side in (0, 1):
                     pass_copy(side, c).wait()
 
-        def apply_rows(c, low, high):
+        def apply_rows(c, r):
             src = slot_of(c, t)
-            total = jnp.dot(poly[low:high, :], x_ref[src], preferred_element_type=F32)
-            x_ref[slot_of(c, t + 1), low:high, :] = (COEF_A * x_ref[src, low:high, :].astype(F32) + total).astype(BF16)
+            total = jnp.dot(poly[r, :], x_ref[src], preferred_element_type=F32)
+            x_ref[slot_of(c, t + 1), r, :] = (COEF_A * x_ref[src, r, :].astype(F32) + total).astype(BF16)
         far_ready(0)
         poly_ready((0, 1, 2))
-        apply_rows(0, 0, BLOCK)
+        apply_rows(0, slice(0, BLOCK))
         pass_weights(W_EARLY, num_chunks)
         poly_ready((3, 4))
-        apply_rows(0, BLOCK, rows)
+        apply_rows(0, slice(BLOCK, tall))
+        apply_rows(0, slice(tall, rows))
 
         @pl.when(t < NS_STEPS - 1)
         def _():
-            def apply_chunk(c, _):
-                far_ready(c)
-                apply_rows(c, 0, rows)
+            def apply_half(q, _):
+                pl.when(lax.rem(q, 2) == 0)(lambda: far_ready(q // 2))
+                apply_rows(q // 2, span(lax.rem(q, 2), tall))
                 return 0
-            lax.fori_loop(1, num_chunks, apply_chunk, 0)
+            lax.fori_loop(2, 2 * num_chunks, apply_half, 0)
 
         @pl.when(t == NS_STEPS - 1)
         def _():
-            def out_pair(q):
+            def out_copy(q, act):
                 c, m = q // 2, lax.rem(q, 2)
-                slot = lax.rem(q, 2)
-                where = wb_ref.at[span(m, tall), columns(core, c)]
-                new = gram.at[span(slot, tall), 0:CHUNK]
-                return (pltpu.make_async_copy(new, where, out_sem.at[slot]),
-                        remote(new, where, out_send.at[slot], out_recv.at[q], partner))
-
-            def row_pair(c):
-                slot = slot_of(c, t + 1)
-                cols = pl.ds(pl.multiple_of(core * half + c * CHUNK, CHUNK), CHUNK)
-                return (pltpu.make_async_copy(x_ref.at[slot, span(me, slab), :], xrow_ref.at[:, cols], row_sem.at[c]),
-                        remote(x_ref.at[slot, span(partner, slab), :], xrow_ref.at[:, cols], row_send.at[c], row_recv.at[c], partner))
-
-            def out_ready(q):
-                tile_load(q).wait()
-
-                @pl.when(q >= 2)
+                new = x_ref.at[slot_of(c, t + 1), span(m, tall), :]
+
+                @pl.when(c < KEPT)
                 def _():
-                    here, there = out_pair(q - 2)
-                    here.wait()
-                    there.wait_send()
+                    act(remote(new, gram.at[span(m, tall), span(c, CHUNK)], out_send.at[q], out_recv.at[q], partner))
+
+                @pl.when((c >= KEPT) & (c < num_chunks - 1))
+                def _():
+                    act(remote(new, wide_ref.at[c - KEPT, span(m, tall), :], out_send.at[q], out_recv.at[q], partner))
+
+                @pl.when(c == num_chunks - 1)
+                def _():
+                    act(remote(new, rest_ref.at[span(m, tall), :], out_send.at[q], out_recv.at[q], partner))
+
+            def kept_rows(which, c):
+                place = which * num_chunks + c
+                return parts.at[4 + place // 2, pl.ds(pl.multiple_of(lax.rem(place, 2) * slab, slab), slab), :]
+
+            def row_copy(c):
+                return remote(parts.at[11, span(lax.rem(c, 2), slab), :], kept_rows(core, c), row_send.at[c], row_recv.at[c], partner)
+
+            def new_rows(c, tile_index, owner):
+                old = parts[tile_index, span(owner, slab), :]
+                ortho = x_ref[slot_of(c, t + 1), span(chip * CORES + owner, slab), :]
+                return decay * old - step_size * ortho.astype(F32)
 
             def new_weight(q):
                 c, m = q // 2, lax.rem(q, 2)
                 slot = lax.rem(q, 2)
+                tile_load(q).wait()
+
+                @pl.when(m == chip // 2)
+                def _():
+                    kept_rows(core, c)[...] = new_rows(c, 2 * slot + lax.rem(chip, 2), core)
+
+                    @pl.when(c >= 2)
+                    def _():
+                        row_copy(c - 2).wait_send()
+                    parts[11, span(lax.rem(c, 2), slab), :] = new_rows(c, 2 * slot + lax.rem(chip, 2), 1 - core)
+                    row_copy(c).start()
                 old = parts[pl.ds(2 * slot, 2)].reshape(tall, CHUNK)
-                ortho = x_ref[slot_of(c, t + 1), span(m, tall), :].astype(F32)
-                new = ((1.0 - LEARN_RATE * WEIGHT_DECAY) * old - (LEARN_RATE * scale) * ortho).astype(BF16)
-                gram[span(slot, tall), 0:CHUNK] = new
-
-            def out_start(q):
-                here, there = out_pair(q)
-                here.start()
-                there.start()
-
-            def last_step(q, _):
-                if NS_STEPS == 1:
-                    pl.when(lax.rem(q, 2) == 0)(lambda: far_ready(q // 2))
-                keep(q, t, apply_value(q, t))
-                out_ready(q)
-                new_weight(q)
-                out_start(q)
-
+                dst = slot_of(c, t + 1)
+                x_ref[dst, span(m, tall), :] = (decay * old - step_size * x_ref[dst, span(m, tall), :].astype(F32)).astype(BF16)
+                out_copy(q, start)
+
+            def next_tile(q):
                 @pl.when(q + 2 < 2 * num_chunks)
                 def _():
                     pl.when(lax.rem(q, 2) == 0)(lambda: w_ready(q // 2 + 1))
                     tile_load(q + 2).start()
 
-                @pl.when(lax.rem(q, 2) == 1)
-                def _():
-                    here, there = row_pair(q // 2)
-                    here.start()
-                    there.start()
+            def last_step(q, _):
+                if NS_STEPS == 1:
+                    pl.when(lax.rem(q, 2) == 0)(lambda: far_ready(q // 2))
+                apply_rows(q // 2, span(lax.rem(q, 2), tall))
+                new_weight(q)
+                next_tile(q)
                 return 0
-            last = 2 * num_chunks - 1
-            for q in (0, 1):
-                out_ready(q)
+
+            def first_tiles(q, _):
                 new_weight(q)
-                out_start(q)
-                if q == 0:
-                    w_ready(1)
-                tile_load(q + 2).start()
-            for copy in row_pair(0):
-                copy.start()
-            lax.fori_loop(2, last + 1, last_step, 0)
-            for q in (last - 1, last):
-                here, there = out_pair(q)
-                here.wait()
-                there.wait_send()
-
-            def out_arrival(q, _):
-                c, m = q // 2, lax.rem(q, 2)
-                where = wb_ref.at[span(m, tall), columns(1 - core, c)]
-                remote(gram.at[0:tall, 0:CHUNK], where, out_send.at[0], out_recv.at[q], partner).wait_recv()
+                next_tile(q)
                 return 0
-            lax.fori_loop(0, 2 * num_chunks, out_arrival, 0)
-
-            def row_end(c, _):
-                here, there = row_pair(c)
-                here.wait()
-                there.wait()
+            lax.fori_loop(0, 2, first_tiles, 0)
+            lax.fori_loop(2, 2 * num_chunks, last_step, 0)
+
+            def out_end(q, _):
+                out_copy(q, lambda copy: copy.wait())
                 return 0
-            lax.fori_loop(0, num_chunks, row_end, 0)
+            lax.fori_loop(0, 2 * num_chunks, out_end, 0)
+            for c in range(num_chunks):
+                if c >= num_chunks - 2:
+                    row_copy(c).wait_send()
+                row_copy(c).wait_recv()
 
         for index in range(5):
             @pl.when((t > 0) & (t < NS_STEPS - 1))
@@ -707,28 +698,31 @@
     lax.fori_loop(0, chips * num_chunks, paired, 0)
 
 
-def hand_over(decay, step, wide_ref, nmom_ref, xrow_ref, w_ref, wide_out, nmom_out, weight_out, wide, nmom, xrow, weight, load_sem, store_sem):
-    count = wide.shape[0]
-    loads = [pltpu.make_async_copy(w_ref, weight, load_sem.at[count]), pltpu.make_async_copy(xrow_ref, xrow, load_sem.at[count + 1])]
-    loads += [pltpu.make_async_copy(nmom_ref, nmom, load_sem.at[count + 2])]
-    loads += [pltpu.make_async_copy(wide_ref.at[i], wide.at[i], load_sem.at[i]) for i in range(count)]
-    stores = [pltpu.make_async_copy(weight, weight_out, store_sem.at[count]), pltpu.make_async_copy(nmom, nmom_out, store_sem.at[count + 2])]
-    stores += [pltpu.make_async_copy(wide.at[i], wide_out.at[i], store_sem.at[i]) for i in range(count)]
-    for load in loads:
-        load.start()
-    loads[0].wait()
-    loads[1].wait()
-
-    def rows_of(i, _):
-        r = span(i, 16)
-        weight[r, :] = decay * weight[r, :] - step * xrow[r, :].astype(F32)
-        return 0
-    lax.fori_loop(0, weight.shape[0] // 16, rows_of, 0)
-    stores[0].start()
-    for load, store in zip(loads[2:], stores[1:]):
-        load.wait()
+def hand_over(half, x_ref, gram, parts, nmom_ref, wide_ref, rest_ref, wide_out, nmom_out, weight_out, rest, wide_sem, load_sem, nmom_sem, weight_sem):
+    core = lax.rem(lax.axis_index('dp'), CORES)
+    slab = nmom_ref.shape[1]
+    num_chunks = half // CHUNK
+    slots = num_chunks + 1
+
+    def columns(which, c):
+        return pl.ds(pl.multiple_of(which * half + c * CHUNK, CHUNK), CHUNK)
+    load = pltpu.make_async_copy(rest_ref, rest, load_sem)
+    load.start()
+    stores = []
+    for c in range(num_chunks):
+        stores.append(pltpu.make_async_copy(x_ref.at[(c + 2 * slots - NS_STEPS) % slots], wide_out.at[:, columns(core, c)], wide_sem.at[0, c]))
+        there = gram.at[:, span(c, CHUNK)] if c < KEPT else wide_ref.at[c - KEPT] if c < num_chunks - 1 else rest
+        stores.append(pltpu.make_async_copy(there, wide_out.at[:, columns(1 - core, c)], wide_sem.at[1, c]))
+    last = stores.pop()
+    for place in range(CORES * num_chunks):
+        where = (slice(None), pl.ds(place * CHUNK, CHUNK))
+        stores.append(pltpu.make_async_copy(nmom_ref.at[place], nmom_out.at[where], nmom_sem.at[place]))
+        stores.append(pltpu.make_async_copy(parts.at[4 + place // 2, pl.ds(place % 2 * slab, slab), :], weight_out.at[where], weight_sem.at[place]))
+    for store in stores:
         store.start()
-    for store in stores:
+    load.wait()
+    last.start()
+    for store in stores + [last]:
         store.wait()
 
 
@@ -748,19 +742,18 @@
 
         def kernel(*refs):
             muon(group, rows, half, scale, *refs)
+        kept = pl.BlockSpec(memory_space=pltpu.VMEM)
         outs = pl.pallas_call(
             kernel,
             name='muon',
-            out_shape=(shape((rows, num_cols), BF16), shape((slab, num_cols), BF16), shape((slab, num_cols), F32),
-                       shape((num_chunks, chips, CORES * slab, CHUNK), F32), shape((chips, slab, num_cols), F32), shape((3, 2, num_chunks, slab, CHUNK), F32)),
+            out_shape=(pltpu.VMEM((num_chunks + 1, rows, CHUNK), BF16), pltpu.VMEM((rows, rows), BF16), pltpu.VMEM((12, BLOCK, BLOCK), F32),
+                       pltpu.VMEM((CORES * num_chunks, slab, CHUNK), F32), pltpu.VMEM((num_chunks - 1 - KEPT, rows, CHUNK), BF16), pltpu.HBM((rows, CHUNK), BF16),
+                       shape((num_chunks, chips, CORES * slab, CHUNK), F32), shape((chips, slab, num_cols), F32),
+                       shape((3, 2, num_chunks, slab, CHUNK), F32)),
             in_specs=[anywhere] * 3,
-            out_specs=(anywhere,) * 6,
+            out_specs=(kept,) * 5 + (anywhere,) * 4,
             scratch_shapes=[
-                pltpu.VMEM((num_chunks + 1, rows, CHUNK), BF16),
                 pltpu.VMEM((rows, rows), BF16),
-                pltpu.VMEM((rows, rows), BF16),
-                pltpu.VMEM((10, BLOCK, BLOCK), F32),
-                pltpu.VMEM((5, BLOCK, BLOCK), F32),
                 pltpu.VMEM((8, CHUNK), F32),
                 pltpu.VMEM((8, 128), F32),
                 pltpu.VMEM((group, 8, 128), F32),
@@ -770,30 +763,25 @@
                 dma((5,)), dma((5,)), dma((5, 2)), dma((5, 2)), dma((5, 2)), dma((5, 2)),
                 dma((2, 2, num_chunks)), dma((2, 2, num_chunks)), dma((2, num_chunks)), dma((2, num_chunks)),
                 dma((num_chunks,)), dma((num_chunks,)), dma((num_chunks,)), dma((2,)),
-                dma((2,)), dma((2,)), dma((2 * num_chunks,)),
-                dma((num_chunks,)), dma((num_chunks,)), dma((num_chunks,)),
+                dma((2 * num_chunks,)), dma((2 * num_chunks,)), dma((num_chunks,)), dma((num_chunks,)),
             ],
-            compiler_params=pltpu.CompilerParams(collective_id=1, has_side_effects=True, vmem_limit_bytes=67043328),
+            compiler_params=pltpu.CompilerParams(collective_id=1, has_side_effects=True, vmem_limit_bytes=VMEM_ROOM),
         )(grad_part[0, 0], momentum[0], weight[0])
-        weight_bf16, ortho, new_momentum = outs[:3]
 
         def last_kernel(*refs):
-            hand_over(1.0 - LEARN_RATE * WEIGHT_DECAY, LEARN_RATE * scale, *refs)
+            hand_over(half, *refs)
         weight_bf16, new_momentum, new_weight = pl.pallas_call(
             last_kernel,
             name='hand_over',
-            out_shape=(shape((group, slab, num_cols), BF16), shape((slab, num_cols), F32), shape((slab, num_cols), F32)),
-            in_specs=[anywhere] * 4,
+            out_shape=(shape((rows, num_cols), BF16), shape((slab, num_cols), F32), shape((slab, num_cols), F32)),
+            in_specs=[kept] * 5 + [pl.BlockSpec(memory_space=pltpu.HBM)],
             out_specs=(anywhere,) * 3,
             scratch_shapes=[
-                pltpu.VMEM((group, slab, num_cols), BF16),
-                pltpu.VMEM((slab, num_cols), F32),
-                pltpu.VMEM((slab, num_cols), BF16),
-                pltpu.VMEM((slab, num_cols), F32),
-                dma((group + 3,)), dma((group + 3,)),
+                pltpu.VMEM((rows, CHUNK), BF16),
+                dma((CORES, num_chunks)), dma(()), dma((CORES * num_chunks,)), dma((CORES * num_chunks,)),
             ],
-            compiler_params=pltpu.CompilerParams(vmem_limit_bytes=56 * 2 ** 20),
-        )(weight_bf16.reshape(group, slab, num_cols), new_momentum, ortho, weight[0])
-        return new_momentum[None], new_weight[None], weight_bf16.reshape(1, rows, num_cols)
+            compiler_params=pltpu.CompilerParams(vmem_limit_bytes=VMEM_ROOM),
+        )(*(pltpu.with_memory_space_constraint(out, pltpu.VMEM) for out in outs[:5]), pltpu.with_memory_space_constraint(outs[5], pltpu.HBM))
+        return new_momentum[None], new_weight[None], weight_bf16[None]
 
     return jax.shard_map(local_step, mesh=mesh, in_specs=(P(('mp', 'dp')), P('mp', 'dp'), P('mp', 'dp')), out_specs=(P('mp', 'dp'), P('mp', 'dp'), P('mp')), check_vma=False)

time: 675 us -> 661 us (0.979)
  Pallas kernels: 673 us -> 660 us
    pallas_call x2, Pallas kernels: 673 us -> 660 us  [the longest x1 645 us: local_step(): pl.pallas_call(kernel, name='muon', out_shape=(pltpu.VMEM((num_chunks + 1...]
where the time goes in v5:
time: 661 us; the launch traced here: 660 us
  Pallas kernels  660 us (100%)
    pallas_call x1, Pallas kernels, local_step(): pl.pallas_call(kernel, name='muon', out_shape=(pltpu.VMEM((num_chunks + 1...  645 us
    pallas_call x1, Pallas kernels, local_step(): pl.pallas_call(last_kernel, name='hand_over', out_shape=(shape((rows, num...  14.5 us

profile of v5, /device:TPU:113, one launch (start us, length us, event | category | flops | bytes accessed | tf_op | source)
XLA Modules:
  0.0 660.3 jit_solution(17198002563619586525)
XLA Ops:
  0.6 645.0 %muon.1 = (bf16[8,2048,512]{2,1,0:T(8,128)(2,1)S(1)}, bf16[2048,2048]{1,0:T(8,128)(2,1)S(1)}, f32[12,512,512]{2,1,0:T(8,128)S(1)}, f32[14,256,512]{2,1,0:T(8,128...) custom-call(f32[2048,7168]{1,0:T(8,128)} %bitcast.6, ...), custom_call_target="tpu_custom_call" | custom-call | tf_op jit(solution)/shard_map/muon/pallas_call | solution.py:746
  645.6 14.5 %hand_over.1 = (bf16[2048,7168]{1,0:T(8,128)(2,1)}, f32[256,7168]{1,0:T(8,128)}, f32[256,7168]{1,0:T(8,128)}) custom-call(bf16[8,2048,512]{2,1,0:T(8,128)(2,1)S(1)} %get-tuple-element.12.refs_0_, bf16[2048,2048]{1,0:T(8,128)(2,1)S(1)} %get-tuple-element.13.refs_1_, f32[12,512,512]{2,1,0:T(8,128)S(1)} %get-tuple-element.14.refs_2_, ...), custom_call_target="tpu_custom_call" | custom-call | tf_op jit(solution)/shard_map/hand_over/pallas_call | solution.py:773

commit v6 on v5

--- a/solution.py
+++ b/solution.py
@@ -21,7 +21,7 @@
 CHUNK = 512
 DEPTH = 4
 KEPT = 4
-VMEM_ROOM = 67 * 2 ** 18
+VMEM_ROOM = 17305 * 2 ** 10
 EAGER = 4
 EARLY = 1
 W_EARLY = 5
@@ -296,13 +296,19 @@
             terms = [lax.dot_general(a, b, ROWS_ROWS, preferred_element_type=F32) for a, b in zip(rows_at(*left), rows_at(*right))]
             return sum(terms[1:], terms[0])
         if diagonal(index):
-            return rows_rows((row, 0, BLOCK), (row, 0, small)), rows_rows((row, small, small), (row, small, small))
+            low = rows_rows((row, small, small), (row, 0, BLOCK))
+            top = rows_rows((row, 0, small), (row, 0, small))
+            return jnp.concatenate([top, low[:, :small]], axis=0), low[:, small:]
         return (rows_rows((row, 0, BLOCK), (col, 0, BLOCK)),)
 
     def pieces_of(ref, value):
         if len(value) == 2:
             return (ref[:, 0:small], ref[small:, small:])
         return (ref[...],)
+
+    def turn_poly(index):
+        row, col = block_of(1 - core, index, SQUARES)
+        poly[span(col, BLOCK), span(row, BLOCK)] = poly[span(row, BLOCK), span(col, BLOCK)].T
 
     def put_block(ref, row, col, value):
         if len(value) == 2:
@@ -341,6 +347,10 @@
         value = lax.dot_general(x_ref[j, span(row, BLOCK), :], x_ref[j, span(col, BLOCK), :], (((1,), (1,)), ((), ())), preferred_element_type=F32)
         slot = place % 3 + 8 * (place // 3)
 
+        if isinstance(j, int):
+            parts[slot] = parts[slot] + value
+            return
+
         @pl.when(j == 0)
         def _():
             parts[slot] = value
@@ -372,7 +382,7 @@
         def _():
             near_copy(place, 1).wait_recv()
 
-    def arrive(j, _):
+    def land(j):
         x_ref[j, rows_of(me), :] = (own(core * num_chunks + j)[...].astype(F32) * inverse).astype(BF16)
         mate_copy(j).wait_recv()
         normalise(j, partner * slab, slab)
@@ -380,6 +390,9 @@
             for from_core in range(CORES):
                 up_copy(side, core, j, from_core).wait_recv()
             normalise(j, side_chip[1 - side] * CORES * slab, CORES * slab)
+
+    def arrive(j, _):
+        land(j)
         for place in range(6):
             near_sum(j, place)
         return 0
@@ -397,22 +410,25 @@
         where = gram.at[span(row, BLOCK), span(col, BLOCK)]
         return remote(where, where, far_send.at[side], far_recv.at[side], side_chip[side] * CORES + core)
 
-    def share_copy(side, owner, b):
+    def share_copy(side, owner):
         row, col = far_block(side_chip[1 - side], owner, side)
-        if b == 1:
-            row, col = col, row
         where = gram.at[span(row, BLOCK), span(col, BLOCK)]
-        return remote(where, where, share_send.at[side, b], share_recv.at[side, b], partner)
-
-    def share(side, owner, act):
-        act(share_copy(side, owner, 0))
+        return remote(where, where, share_send.at[side], share_recv.at[side], partner)
+
+    def turn(side, owner):
         row, col = far_block(side_chip[1 - side], owner, side)
 
         @pl.when(row != col)
         def _():
-            act(share_copy(side, owner, 1))
-
-    lax.fori_loop(0, num_chunks, arrive, 0)
+            gram[span(col, BLOCK), span(row, BLOCK)] = gram[span(row, BLOCK), span(col, BLOCK)].T
+
+    lax.fori_loop(0, num_chunks - 1, arrive, 0)
+    land(num_chunks - 1)
+    for place in range(3):
+        near_sum(num_chunks - 1, place)
+        part_copy(place).start()
+    for place in range(3, 6):
+        near_sum(num_chunks - 1, place)
 
     def sent(j, _):
         for side in (0, 1):
@@ -422,8 +438,6 @@
         return 0
     lax.fori_loop(0, num_chunks, sent, 0)
 
-    for place in range(3):
-        part_copy(place).start()
 
     for c in range(EARLY):
         for side in (0, 1):
@@ -456,17 +470,15 @@
         near_arrived(place)
     for side in (0, 1):
         far_copy(side).wait_recv()
-        row, col = far_block(side_chip[1 - side], core, side)
-        turned = gram[span(row, BLOCK), span(col, BLOCK)].T
-
-        @pl.when(row != col)
-        def _():
-            gram[span(col, BLOCK), span(row, BLOCK)] = turned
-        share(side, core, start)
+        share_copy(side, core).start()
     for side in (0, 1):
-        share(side, 1 - core, arrived)
+        turn(side, core)
+    for side in (0, 1):
+        share_copy(side, 1 - core).wait_recv()
+        turn(side, 1 - core)
+    for side in (0, 1):
         far_copy(side).wait_send()
-        share(side, core, left)
+        share_copy(side, core).wait_send()
     for place in range(3):
         near_both(place, left)
         part_copy(place).wait_send()
@@ -525,18 +537,26 @@
             lax.fori_loop(2, 4, gram_middle, 0)
         alone(gram_own, 4)
 
+        def once(owner, index, act):
+            row, col = block_of(owner, index, SQUARES)
+            act(poly_copy(0, index, row, col))
+
         def squares(indices, needs):
             @pl.when(t > 0)
             def _():
                 for index in needs:
                     both(gram_copy, 1 - core, index, arrived)
+            if 4 in indices:
+                once(1 - core, 1, arrived)
             for index in indices:
                 row, col = block_of(core, index, SQUARES)
                 value = product(gram_rows, index, row, col)
                 old = pieces_of(gram.at[span(row, BLOCK), span(col, BLOCK)], value)
                 put_block(poly, row, col, tuple(COEF_B * g.astype(F32) + COEF_C * v for g, v in zip(old, value)))
+                if index == 4:
+                    turn_poly(1)
             for index in indices:
-                both(poly_copy, core, index, start, SQUARES)
+                once(core, index, start)
         def part_drain(i, carry):
             part_copy(i).wait_send()
             return carry
@@ -563,10 +583,6 @@
             w_ready(0)
             tile_load(0).start()
             tile_load(1).start()
-
-        def poly_ready(indices):
-            for index in indices:
-                both(poly_copy, 1 - core, index, arrived, SQUARES)
 
         def far_ready(c):
             @pl.when(t == 0)
@@ -579,20 +595,25 @@
             total = jnp.dot(poly[r, :], x_ref[src], preferred_element_type=F32)
             x_ref[slot_of(c, t + 1), r, :] = (COEF_A * x_ref[src, r, :].astype(F32) + total).astype(BF16)
         far_ready(0)
-        poly_ready((0, 1, 2))
+        once(1 - core, 0, arrived)
+        once(1 - core, 2, arrived)
+        turn_poly(2)
+        once(1 - core, 3, arrived)
+        turn_poly(3)
         apply_rows(0, slice(0, BLOCK))
         pass_weights(W_EARLY, num_chunks)
-        poly_ready((3, 4))
+        once(1 - core, 4, arrived)
         apply_rows(0, slice(BLOCK, tall))
         apply_rows(0, slice(tall, rows))
 
         @pl.when(t < NS_STEPS - 1)
         def _():
-            def apply_half(q, _):
-                pl.when(lax.rem(q, 2) == 0)(lambda: far_ready(q // 2))
-                apply_rows(q // 2, span(lax.rem(q, 2), tall))
+            def apply_chunk(c, _):
+                far_ready(c)
+                for half_rows in range(2):
+                    apply_rows(c, slice(half_rows * tall, (half_rows + 1) * tall))
                 return 0
-            lax.fori_loop(2, 2 * num_chunks, apply_half, 0)
+            lax.fori_loop(1, num_chunks, apply_chunk, 0)
 
         @pl.when(t == NS_STEPS - 1)
         def _():
@@ -677,7 +698,7 @@
             @pl.when((t > 0) & (t < NS_STEPS - 1))
             def _():
                 both(gram_copy, core, index, left)
-            both(poly_copy, core, index, left, SQUARES)
+            once(core, index, left)
         return 0
     lax.fori_loop(0, NS_STEPS, step, 0)
 
@@ -759,7 +780,7 @@
                 pltpu.VMEM((group, 8, 128), F32),
                 dma((chips * num_chunks * 2,)), dma((chips * num_chunks * 2,)), dma((2, DEPTH)), dma((3, 2, num_chunks)), dma((6,)),
                 dma((group,)), dma((group,)), dma((2, 2, num_chunks)), dma((2, 2, num_chunks)), dma((num_chunks,)), dma((num_chunks,)),
-                dma((2, num_chunks)), dma((2, num_chunks)), dma((2,)), dma((2,)), dma((2, 2)), dma((2, 2)),
+                dma((2, num_chunks)), dma((2, num_chunks)), dma((2,)), dma((2,)), dma((2,)), dma((2,)),
                 dma((5,)), dma((5,)), dma((5, 2)), dma((5, 2)), dma((5, 2)), dma((5, 2)),
                 dma((2, 2, num_chunks)), dma((2, 2, num_chunks)), dma((2, num_chunks)), dma((2, num_chunks)),
                 dma((num_chunks,)), dma((num_chunks,)), dma((num_chunks,)), dma((2,)),

time: 661 us -> 658 us (level)
  no operation moved by 1% of the time
where the time goes in v6:
time: 658 us; the launch traced here: 657 us
  Pallas kernels  656 us (100%)
    pallas_call x1, Pallas kernels, local_step(): pl.pallas_call(kernel, name='muon', out_shape=(pltpu.VMEM((num_chunks + 1...  642 us
    pallas_call x1, Pallas kernels, local_step(): pl.pallas_call(last_kernel, name='hand_over', out_shape=(shape((rows, num...  14.5 us

profile of v6, /device:TPU:113, one launch (start us, length us, event | category | flops | bytes accessed | tf_op | source)
XLA Modules:
  0.0 657.2 jit_solution(1258964337796313951)
XLA Ops:
  0.6 641.8 %muon.1 = (bf16[8,2048,512]{2,1,0:T(8,128)(2,1)S(1)}, bf16[2048,2048]{1,0:T(8,128)(2,1)S(1)}, f32[12,512,512]{2,1,0:T(8,128)S(1)}, f32[14,256,512]{2,1,0:T(8,128...) custom-call(f32[2048,7168]{1,0:T(8,128)} %bitcast.6, ...), custom_call_target="tpu_custom_call" | custom-call | tf_op jit(solution)/shard_map/muon/pallas_call | solution.py:767
  642.5 14.5 %hand_over.1 = (bf16[2048,7168]{1,0:T(8,128)(2,1)}, f32[256,7168]{1,0:T(8,128)}, f32[256,7168]{1,0:T(8,128)}) custom-call(bf16[8,2048,512]{2,1,0:T(8,128)(2,1)S(1)} %get-tuple-element.12.refs_0_, bf16[2048,2048]{1,0:T(8,128)(2,1)S(1)} %get-tuple-element.13.refs_1_, f32[12,512,512]{2,1,0:T(8,128)S(1)} %get-tuple-element.14.refs_2_, ...), custom_call_target="tpu_custom_call" | custom-call | tf_op jit(solution)/shard_map/hand_over/pallas_call | solution.py:794

commit v7 on v6

--- a/solution.py
+++ b/solution.py
@@ -21,7 +21,7 @@
 CHUNK = 512
 DEPTH = 4
 KEPT = 4
-VMEM_ROOM = 17305 * 2 ** 10
+VMEM_ROOM = 17216 * 2 ** 10
 EAGER = 4
 EARLY = 1
 W_EARLY = 5
@@ -541,6 +541,8 @@
             row, col = block_of(owner, index, SQUARES)
             act(poly_copy(0, index, row, col))
 
+        always = jnp.minimum(t + 1, 1)
+
         def squares(indices, needs):
             @pl.when(t > 0)
             def _():
@@ -548,13 +550,17 @@
                     both(gram_copy, 1 - core, index, arrived)
             if 4 in indices:
                 once(1 - core, 1, arrived)
-            for index in indices:
-                row, col = block_of(core, index, SQUARES)
-                value = product(gram_rows, index, row, col)
-                old = pieces_of(gram.at[span(row, BLOCK), span(col, BLOCK)], value)
-                put_block(poly, row, col, tuple(COEF_B * g.astype(F32) + COEF_C * v for g, v in zip(old, value)))
-                if index == 4:
-                    turn_poly(1)
+
+            def take(_, carry):
+                for index in indices:
+                    row, col = block_of(core, index, SQUARES)
+                    value = product(gram_rows, index, row, col)
+                    old = pieces_of(gram.at[span(row, BLOCK), span(col, BLOCK)], value)
+                    put_block(poly, row, col, tuple(COEF_B * g.astype(F32) + COEF_C * v for g, v in zip(old, value)))
+                    if index == 4:
+                        turn_poly(1)
+                return carry
+            lax.fori_loop(0, always, take, None)
             for index in indices:
                 once(core, index, start)
         def part_drain(i, carry):
@@ -563,8 +569,7 @@
         pl.when(t > 0)(lambda: lax.fori_loop(0, 5, part_drain, None))
 
         squares((0,), (0, 1, 2))
-        squares((1,), (3,))
-        squares((2,), ())
+        squares((1, 2), (3,))
         squares((3,), (4,))
 
         @pl.when((t == NS_STEPS - 1) & (t > 0))

time: 658 us -> 655 us (level)
  no operation moved by 1% of the time
where the time goes in v7:
time: 655 us
  Pallas kernels  654 us (100%)
    pallas_call x1, Pallas kernels, local_step(): pl.pallas_call(kernel, name='muon', out_shape=(pltpu.VMEM((num_chunks + 1...  639 us
    pallas_call x1, Pallas kernels, local_step(): pl.pallas_call(last_kernel, name='hand_over', out_shape=(shape((rows, num...  14.5 us

profile of v7, /device:TPU:113, one launch (start us, length us, event | category | flops | bytes accessed | tf_op | source)
XLA Modules:
  0.0 654.6 jit_solution(2740157881371800027)
XLA Ops:
  0.6 639.3 %muon.1 = (bf16[8,2048,512]{2,1,0:T(8,128)(2,1)S(1)}, bf16[2048,2048]{1,0:T(8,128)(2,1)S(1)}, f32[12,512,512]{2,1,0:T(8,128)S(1)}, f32[14,256,512]{2,1,0:T(8,128...) custom-call(f32[2048,7168]{1,0:T(8,128)} %bitcast.6, ...), custom_call_target="tpu_custom_call" | custom-call | tf_op jit(solution)/shard_map/muon/pallas_call | solution.py:772
  639.9 14.5 %hand_over.1 = (bf16[2048,7168]{1,0:T(8,128)(2,1)}, f32[256,7168]{1,0:T(8,128)}, f32[256,7168]{1,0:T(8,128)}) custom-call(bf16[8,2048,512]{2,1,0:T(8,128)(2,1)S(1)} %get-tuple-element.12.refs_0_, bf16[2048,2048]{1,0:T(8,128)(2,1)S(1)} %get-tuple-element.13.refs_1_, f32[12,512,512]{2,1,0:T(8,128)S(1)} %get-tuple-element.14.refs_2_, ...), custom_call_target="tpu_custom_call" | custom-call | tf_op jit(solution)/shard_map/hand_over/pallas_call | solution.py:799
